TPU v7x, 32 devices: a whole 2x2x4 slice. The times are simulated.
32 devices in a mesh: fr: 2 (over core), sr: 4 (over z), sc: 4 (over y, x).
Axes of the slice: x: 2, y: 2, z: 4, core: 2. Of those that a mesh axis runs over, the one named last changes fastest.
Arguments:
- spec_re: bfloat16 [8, 2048, 256], P('fr', ('sr', 'sc')), may hold values from -6 to 6
- spec_im: bfloat16 [8, 2048, 256], P('fr', ('sr', 'sc')), may hold values from -6 to 6
- offsets: int32 [16, 9], P(('sr', 'sc')), may hold values from 0 to 8, each once within a row
Outputs:
- cross: float32 [8, 16, 9, 128, 256], P('fr', ('sr', 'sc'))
Inputs may be any that keep to these rules, and one draw needn't show every extreme that they name: Each row of offsets names every offset 0 to 8 exactly once.
All inputs are finite; a program needn't handle non-finite values.
Results may differ from a plain program's by a relative error of at most 0.0003.
Values may be sent and summed in bfloat16 or wider, within the bound.
No kernel may reach another device: no remote copies, remote signals or barrier semaphores. Data moves between devices by JAX's collectives and lax.ppermute only.
A program may use at most 128 MiB of HBM per device.

v0:
```python
import functools
import math

import jax
import jax.numpy as jnp
from jax import lax
from jax.experimental import pallas as pl
from jax.experimental.pallas import tpu as pltpu
from jax.sharding import PartitionSpec as P


BLOCKS = ("sr", "sc")
GAIN_PARTS = 3
GAIN_ROWS = 16
VMEM_BYTES = 16 << 20


def product_kernel(entries, offsets_ref, re_ref, im_ref, weight_ref, *refs):
    pair_count = len(entries)
    reals = refs[:pair_count]
    imags = refs[pair_count : 2 * pair_count]
    out_ref, stage, sems = refs[-3:]
    bins, rows, _ = re_ref.shape
    slot_count = offsets_ref.shape[1]
    contract = (((1,), (1,)), ((), ()))
    column = lax.axis_index("sc")

    wanted, slots = [], []
    for entry in entries:
        offset, use = entry(column)
        use = jnp.logical_and(use, jnp.logical_and(offset >= 0, offset < slot_count))

        def find(m, found, offset=offset):
            return jnp.where(offsets_ref[0, m] == offset, m, found)

        wanted.append(use)
        slots.append(lax.fori_loop(0, slot_count, find, jnp.int32(0), unroll=True))

    def copy_out(i, f):
        return pltpu.make_async_copy(
            stage.at[i, f], out_ref.at[f, 0, slots[i]], sems.at[i, f]
        )

    for i in range(pair_count):

        @pl.when(wanted[i])
        def _(i=i):
            parts = imags[i][pl.ds(bins * rows, GAIN_ROWS), :rows].astype(jnp.float32)
            gain = parts[0:1] + parts[1:2] + parts[2:3]
            weight = weight_ref[...] * gain

            for f in range(bins):
                own = jnp.concatenate([re_ref[f], im_ref[f]], axis=0)
                turned = jnp.concatenate([im_ref[f], -re_ref[f]], axis=0)
                other_re = reals[i][f]
                other_im = imags[i][pl.ds(f * rows, rows), :]
                first = lax.dot_general(
                    own, other_re, contract, preferred_element_type=jnp.float32
                )
                second = lax.dot_general(
                    turned, other_im, contract, preferred_element_type=jnp.float32
                )
                both = first + second
                stage[i, f, :, :rows] = both[:rows] * weight
                stage[i, f, :, rows:] = both[rows:] * weight
                copy_out(i, f).start()

    for i in range(pair_count):

        @pl.when(wanted[i])
        def _(i=i):
            for f in range(bins):
                copy_out(i, f).wait()


def products(offsets, re_own, im_own, weight, group, out_shape, out):
    bins, rows, segs = re_own.shape
    count = len(group)
    vmem = pl.BlockSpec(memory_space=pltpu.VMEM)
    args = [offsets, re_own, im_own, weight]
    args += [pair[0] for pair, _ in group] + [pair[1] for pair, _ in group]
    specs = [pl.BlockSpec(memory_space=pltpu.SMEM)] + [vmem] * (len(args) - 1)
    aliases = {}
    if out is not None:
        aliases = {len(args): 0}
        args.append(out)
        specs.append(pl.BlockSpec(memory_space=pl.ANY))
    tile_bytes = rows * 2 * rows * 4
    return pl.pallas_call(
        functools.partial(product_kernel, [entry for _, entry in group]),
        out_shape=out_shape,
        in_specs=specs,
        out_specs=pl.BlockSpec(memory_space=pl.ANY),
        scratch_shapes=[
            pltpu.VMEM((count, bins, rows, 2 * rows), jnp.float32),
            pltpu.SemaphoreType.DMA((count, bins)),
        ],
        input_output_aliases=aliases,
        compiler_params=pltpu.CompilerParams(vmem_limit_bytes=VMEM_BYTES),
        cost_estimate=pl.CostEstimate(
            flops=count * bins * 8 * rows * rows * segs,
            bytes_accessed=count * bins * tile_bytes,
            transcendentals=0,
        ),
    )(*args)


def local(sr, sc, spec_re, spec_im, offsets):
    bins, rows, segs = spec_re.shape
    slot_count = offsets.shape[1]
    half = sr // 2
    bin_total = bins * lax.axis_size("fr")
    column = lax.axis_index("sc")
    norm = 1.0 / math.sqrt(segs)

    def send(value, route):
        links = []
        for z in range(sr):
            for s in range(sc):
                target = route(z, s)
                if target is not None:
                    links.append((z * sc + s, (target[0] % sr) * sc + target[1]))
        return lax.ppermute(value, BLOCKS, links)

    def both(pair, route):
        return send(pair[0], route), send(pair[1], route)

    everyone = range(sc)
    upper = [s for s in everyone if s & 2]
    lower = [s for s in everyone if not s & 2]
    odd = [s for s in everyone if s & 1]

    def down(columns=everyone):
        return lambda z, s: (z - 1, s) if s in columns else None

    def flip(bit, columns=everyone):
        return lambda z, s: (z, s ^ bit) if s in columns else None

    re32 = spec_re.astype(jnp.float32)
    im32 = spec_im.astype(jnp.float32)
    power_half = jnp.sum(re32 * re32 + im32 * im32, axis=(0, 2))
    power_other = lax.ppermute(power_half, "fr", [(0, 1), (1, 0)])
    gain = lax.rsqrt((power_half + power_other) / (bin_total * segs))
    parts, rest = [], gain
    for _ in range(GAIN_PARTS):
        part = lax.reduce_precision(rest, exponent_bits=8, mantissa_bits=7)
        parts.append(part)
        rest = rest - part
    tail = jnp.stack(parts).astype(jnp.bfloat16)
    tail = jnp.pad(tail, ((0, GAIN_ROWS - GAIN_PARTS), (0, segs - rows)))
    weight = jnp.broadcast_to((gain * norm)[:, None], (rows, rows))
    own = (spec_re, jnp.concatenate([spec_im.reshape(bins * rows, segs), tail], axis=0))

    planes = [own]
    for _ in range(half):
        planes.append(both(planes[-1], down()))
    near, far = planes[half - 1], planes[half]
    u1, u2 = both(own, flip(1, odd)), both(near, flip(1))
    v1, v2 = both(own, flip(2, upper)), both(near, flip(2))
    is_upper = (column & 2) != 0
    x3 = tuple(send(jnp.where(is_upper, v2[h], v1[h]), flip(1)) for h in range(2))
    y3 = tuple(send(jnp.where(is_upper, u2[h], far[h]), flip(2)) for h in range(2))
    z3b = send(u2[1], down([0, 1, 3]))
    late, early = lax.optimization_barrier((x3[0], u2[0]))
    z3a = send(jnp.where(column == 2, late, early), down([1, 2, 3]))
    xfa = send(y3[0], flip(1, [2]))
    yfb = send(z3b, flip(2, lower))

    def entry(plane, bit, use=lambda column: True):
        return lambda column: (plane * sc + (column ^ bit) - column, use(column))

    def x3_entry(column):
        plane = jnp.where((column & 2) != 0, half - 1, 0)
        return plane * sc + (column ^ 3) - column, True

    def y3_entry(column):
        is_upper = (column & 2) != 0
        plane = jnp.where(is_upper, half, half - 1)
        return plane * sc + (column ^ jnp.where(is_upper, 2, 3)) - column, True

    groups = [
        [(own, entry(0, 0)), (near, entry(half - 1, 0)), (u1, entry(0, 1)), (v1, entry(0, 2))],
        [(u2, entry(half - 1, 1)), (v2, entry(half - 1, 2)), (far, entry(half, 0))],
    ]
    for j in range(1, half - 1):
        u = both(planes[j], flip(1))
        v = both(planes[j], flip(2))
        d = both(v, flip(1))
        groups.append([(p, entry(j, bit)) for bit, p in enumerate((planes[j], u, v, d))])
    groups.append(
        [
            (x3, x3_entry),
            (y3, y3_entry),
            ((z3a, z3b), entry(half, 1, lambda column: (column & 1) == 1)),
            ((z3a, yfb), entry(half, 3, lambda column: column == 2)),
            ((xfa, yfb), entry(half, 3, lambda column: column == 3)),
        ]
    )
    out_shape = jax.ShapeDtypeStruct((bins, 1, slot_count, rows, 2 * rows), jnp.float32)
    out = None
    for group in groups:
        out = products(offsets, spec_re, spec_im, weight, group, out_shape, out)
    return out


def solution(mesh):
    sr, sc = mesh.shape["sr"], mesh.shape["sc"]
    placed = (P("fr", ("sr", "sc"), None), P("fr", ("sr", "sc"), None), P(("sr", "sc"), None))

    def body(*args):
        return local(sr, sc, *args)

    return jax.shard_map(
        body,
        mesh=mesh,
        in_specs=placed,
        out_specs=P("fr", ("sr", "sc"), None, None, None),
        check_vma=False,
    )
```

profile of v0, /device:TPU:4, one launch (start us, length us, event | category | flops | bytes accessed | tf_op | source)
XLA Modules:
  0.0 61.5 jit_solution(15746576071011053176)
XLA Ops:
  0.0 1.3 %add_reduce_fusion = f32[128]{0:T(128)S(1)} fusion(bf16[4,128,256]{2,1,0:T(8,128)(2,1)} %im_ref.5, bf16[4,128,256]{2,1,0:T(8,128)(2,1)} %re_ref.5), kind=kLoop, calls=%fused_computation | loop fusion | flops 786304 | bytes 524800 | tf_op jit(solution)/shard_map/reduce_sum | solution.py:141
  1.3 0.1 collective-permute-start
  1.4 3.7 %collective-permute-start.1 = (bf16[4,128,256]{2,1,0:T(8,128)(2,1)}, bf16[4,128,256]{2,1,0:T(8,128)(2,1)S(1)}, u32[]{:S(2)}, u32[]{:S(2)}) collective-permute-start(bf16[4,128,256]{2,1,0:T(8,128)(2,1)} %re_ref.5), channel_id=1, source_target_pairs={{0,12},{1,13},{2,14},{3,15},{4,0},{5,1},{6,2},{7,3},{8,4},{9,5},{1... | collective-permute-start | bytes 786440 | tf_op jit(solution)/shard_map/ppermute | solution.py:123
  5.0 0.0 collective-permute-done
  5.1 1.0 %pad_maximum_fusion.refs_4_ = bf16[528,256]{1,0:T(8,128)(2,1)S(1)} fusion(bf16[16,256]{1,0:T(8,128)(2,1)S(1)} %fusion.8, bf16[512,256]{1,0:T(8,128)(2,1)} %bitcast.7), kind=kLoop, calls=%fused_computation.1 | loop fusion | flops 540672 | bytes 540672 | tf_op jit(solution)/shard_map/concatenate | solution.py:152
  6.0 1.1 %collective-permute-start.10 = (bf16[528,256]{1,0:T(8,128)(2,1)S(1)}, bf16[528,256]{1,0:T(8,128)(2,1)S(1)}, u32[]{:S(2)}, u32[]{:S(2)}) collective-permute-start(bf16[528,256]{1,0:T(8,128)(2,1)S(1)} %pad_maximum_fusion.refs_4_), channel_id=1, source_target_pairs={{0,12},{1,13},{2,14},{3,15},{4,0},{5,1},{6,2},{7,3},{8,4},{9,5},{1... | collective-permute-start | bytes 811016 | tf_op jit(solution)/shard_map/ppermute | solution.py:123
  7.2 2.4 %collective-permute-start.3 = (bf16[4,128,256]{2,1,0:T(8,128)(2,1)}, bf16[4,128,256]{2,1,0:T(8,128)(2,1)S(1)}, u32[]{:S(2)}, u32[]{:S(2)}) collective-permute-start(bf16[4,128,256]{2,1,0:T(8,128)(2,1)} %re_ref.5), channel_id=1, source_target_pairs={{2,0},{3,1},{6,4},{7,5},{10,8},{11,9},{14,12},{15,13},{18,16},{19,... | collective-permute-start | bytes 786440 | tf_op jit(solution)/shard_map/ppermute | solution.py:123
  9.6 2.4 %collective-permute-done.1.refs_1_ = bf16[4,128,256]{2,1,0:T(8,128)(2,1)S(1)} collective-permute-done((bf16[4,128,256]{2,1,0:T(8,128)(2,1)}, bf16[4,128,256]{2,1,0:T(8,128)(2,1)S(1)}, u32[]{:S(2)}, u32[]{:S(2)}) %collective-permute-start.1) | collective-permute-done | bytes 262176 | tf_op jit(solution)/shard_map/ppermute | solution.py:123
  12.0 0.5 collective-permute-start.2
  12.5 1.5 %collective-permute-start.5 = (bf16[4,128,256]{2,1,0:T(8,128)(2,1)S(1)}, bf16[4,128,256]{2,1,0:T(8,128)(2,1)S(1)}, u32[]{:S(2)}, u32[]{:S(2)}) collective-permute-start(bf16[4,128,256]{2,1,0:T(8,128)(2,1)S(1)} %collective-permute-done.1.refs_1_), channel_id=1, source_target_pairs={{0,1},{1,0},{2,3},{3,2},{4,5},{5,4},{6,7},{7,6},{8,9},{9,8},{10,11... | collective-permute-start | bytes 786440 | tf_op jit(solution)/shard_map/ppermute | solution.py:123
  14.0 4.2 %collective-permute-start.6 = (bf16[4,128,256]{2,1,0:T(8,128)(2,1)S(1)}, bf16[4,128,256]{2,1,0:T(8,128)(2,1)S(1)}, u32[]{:S(2)}, u32[]{:S(2)}) collective-permute-start(bf16[4,128,256]{2,1,0:T(8,128)(2,1)S(1)} %collective-permute-done.1.refs_1_), channel_id=1, source_target_pairs={{0,12},{1,13},{2,14},{3,15},{4,0},{5,1},{6,2},{7,3},{8,4},{9,5},{1... | collective-permute-start | bytes 786440 | tf_op jit(solution)/shard_map/ppermute | solution.py:123
  18.2 0.0 collective-permute-done.3.refs_3_
  18.2 1.3 %collective-permute-start.19 = (bf16[4,128,256]{2,1,0:T(8,128)(2,1)}, bf16[4,128,256]{2,1,0:T(8,128)(2,1)S(1)}, u32[]{:S(2)}, u32[]{:S(2)}) collective-permute-start(bf16[4,128,256]{2,1,0:T(8,128)(2,1)} %re_ref.5), channel_id=1, source_target_pairs={{1,0},{3,2},{5,4},{7,6},{9,8},{11,10},{13,12},{15,14},{17,16},{19,... | collective-permute-start | bytes 786440 | tf_op jit(solution)/shard_map/ppermute | solution.py:123
  19.5 0.0 collective-permute-done.10.refs_5_
  19.5 2.7 %collective-permute-start.14 = (bf16[528,256]{1,0:T(8,128)(2,1)S(1)}, bf16[528,256]{1,0:T(8,128)(2,1)S(1)}, u32[]{:S(2)}, u32[]{:S(2)}) collective-permute-start(bf16[528,256]{1,0:T(8,128)(2,1)S(1)} %collective-permute-done.10.refs_5_), channel_id=1, source_target_pairs={{0,1},{1,0},{2,3},{3,2},{4,5},{5,4},{6,7},{7,6},{8,9},{9,8},{10,11... | collective-permute-start | bytes 811016 | tf_op jit(solution)/shard_map/ppermute | solution.py:123
  22.2 0.0 collective-permute-done.2.refs_1_
  22.2 1.3 %collective-permute-start.15 = (bf16[528,256]{1,0:T(8,128)(2,1)S(1)}, bf16[528,256]{1,0:T(8,128)(2,1)S(1)}, u32[]{:S(2)}, u32[]{:S(2)}) collective-permute-start(bf16[528,256]{1,0:T(8,128)(2,1)S(1)} %collective-permute-done.10.refs_5_), channel_id=1, source_target_pairs={{0,12},{1,13},{2,14},{3,15},{4,0},{5,1},{6,2},{7,3},{8,4},{9,5},{1... | collective-permute-start | bytes 811016 | tf_op jit(solution)/shard_map/ppermute | solution.py:123
  23.5 0.0 collective-permute-done.5.refs_0_
  23.5 2.4 %collective-permute-start.12 = (bf16[528,256]{1,0:T(8,128)(2,1)S(1)}, bf16[528,256]{1,0:T(8,128)(2,1)S(1)}, u32[]{:S(2)}, u32[]{:S(2)}) collective-permute-start(bf16[528,256]{1,0:T(8,128)(2,1)S(1)} %pad_maximum_fusion.refs_4_), channel_id=1, source_target_pairs={{2,0},{3,1},{6,4},{7,5},{10,8},{11,9},{14,12},{15,13},{18,16},{19,... | collective-permute-start | bytes 811016 | tf_op jit(solution)/shard_map/ppermute | solution.py:123
  25.9 0.0 collective-permute-done.6.refs_2_
  26.0 0.1 collective-permute-start.11
  26.1 6.5 %collective-permute-done.14.refs_3_ = bf16[528,256]{1,0:T(8,128)(2,1)S(1)} collective-permute-done((bf16[528,256]{1,0:T(8,128)(2,1)S(1)}, bf16[528,256]{1,0:T(8,128)(2,1)S(1)}, u32[]{:S(2)}, u32[]{:S(2)}) %collective-permute-start.14) | collective-permute-done | bytes 270368 | tf_op jit(solution)/shard_map/ppermute | solution.py:123
  32.6 0.0 collective-permute-start.4
  32.6 0.0 collective-permute-done.15.refs_5_
  32.6 0.7 %collective-permute-start.17 = (bf16[528,256]{1,0:T(8,128)(2,1)S(1)}, bf16[528,256]{1,0:T(8,128)(2,1)S(1)}, u32[]{:S(2)}, u32[]{:S(2)}) collective-permute-start(bf16[528,256]{1,0:T(8,128)(2,1)S(1)} %collective-permute-done.14.refs_3_), channel_id=1, source_target_pairs={{0,12},{1,13},{3,15},{4,0},{5,1},{7,3},{8,4},{9,5},{11,7},{12,8},{... | collective-permute-start | bytes 811016 | tf_op jit(solution)/shard_map/ppermute | solution.py:123
  33.3 0.0 collective-permute-done.12.refs_7_
  33.3 1.3 %collective-permute-start.20 = (bf16[528,256]{1,0:T(8,128)(2,1)S(1)}, bf16[528,256]{1,0:T(8,128)(2,1)S(1)}, u32[]{:S(2)}, u32[]{:S(2)}) collective-permute-start(bf16[528,256]{1,0:T(8,128)(2,1)S(1)} %pad_maximum_fusion.refs_4_), channel_id=1, source_target_pairs={{1,0},{3,2},{5,4},{7,6},{9,8},{11,10},{13,12},{15,14},{17,16},{19,... | collective-permute-start | bytes 811016 | tf_op jit(solution)/shard_map/ppermute | solution.py:123
  34.6 1.6 %collective-permute-done.11.refs_4_ = bf16[528,256]{1,0:T(8,128)(2,1)S(1)} collective-permute-done((bf16[528,256]{1,0:T(8,128)(2,1)S(1)}, bf16[528,256]{1,0:T(8,128)(2,1)S(1)}, u32[]{:S(2)}, u32[]{:S(2)}) %collective-permute-start.11) | collective-permute-done | bytes 270368 | tf_op jit(solution)/shard_map/ppermute | solution.py:123
  36.2 3.8 %collective-permute-start.7 = (bf16[4,128,256]{2,1,0:T(8,128)(2,1)S(1)}, bf16[4,128,256]{2,1,0:T(8,128)(2,1)S(1)}, u32[]{:S(2)}, u32[]{:S(2)}) collective-permute-start(bf16[4,128,256]{2,1,0:T(8,128)(2,1)S(1)} %broadcast_select_fusion.3), channel_id=1, source_target_pairs={{0,2},{1,3},{2,0},{3,1},{4,6},{5,7},{6,4},{7,5},{8,10},{9,11},{10,... | collective-permute-start | bytes 786440 | tf_op jit(solution)/shard_map/ppermute | solution.py:123
  40.0 0.0 collective-permute-done.4.refs_0_
  40.0 0.4 collective-permute-start.16
  40.4 0.0 collective-permute-done.19.refs_2_
  40.5 2.4 %collective-permute-start.13 = (bf16[528,256]{1,0:T(8,128)(2,1)S(1)}, bf16[528,256]{1,0:T(8,128)(2,1)S(1)}, u32[]{:S(2)}, u32[]{:S(2)}) collective-permute-start(bf16[528,256]{1,0:T(8,128)(2,1)S(1)} %broadcast_select_fusion.1), channel_id=1, source_target_pairs={{0,1},{1,0},{2,3},{3,2},{4,5},{5,4},{6,7},{7,6},{8,9},{9,8},{10,11... | collective-permute-start | bytes 811016 | tf_op jit(solution)/shard_map/ppermute | solution.py:123
  42.8 0.0 collective-permute-done.17.refs_7_
  42.8 1.3 %collective-permute-start.18 = (bf16[528,256]{1,0:T(8,128)(2,1)S(1)}, bf16[528,256]{1,0:T(8,128)(2,1)S(1)}, u32[]{:S(2)}, u32[]{:S(2)}) collective-permute-start(bf16[528,256]{1,0:T(8,128)(2,1)S(1)} %collective-permute-done.17.refs_7_), channel_id=1, source_target_pairs={{0,2},{1,3},{4,6},{5,7},{8,10},{9,11},{12,14},{13,15},{16,18},{17,... | collective-permute-start | bytes 811016 | tf_op jit(solution)/shard_map/ppermute | solution.py:123
  44.2 3.5 %collective-permute-done.20.refs_6_ = bf16[528,256]{1,0:T(8,128)(2,1)S(1)} collective-permute-done((bf16[528,256]{1,0:T(8,128)(2,1)S(1)}, bf16[528,256]{1,0:T(8,128)(2,1)S(1)}, u32[]{:S(2)}, u32[]{:S(2)}) %collective-permute-start.20) | collective-permute-done | bytes 270368 | tf_op jit(solution)/shard_map/ppermute | solution.py:123
  47.6 4.1 %collective-permute-start.8 = (bf16[4,128,256]{2,1,0:T(8,128)(2,1)S(1)}, bf16[4,128,256]{2,1,0:T(8,128)(2,1)S(1)}, u32[]{:S(2)}, u32[]{:S(2)}) collective-permute-start(bf16[4,128,256]{2,1,0:T(8,128)(2,1)S(1)} %broadcast_select_fusion.2), channel_id=1, source_target_pairs={{1,13},{2,14},{3,15},{5,1},{6,2},{7,3},{9,5},{10,6},{11,7},{13,9},... | collective-permute-start | bytes 786440 | tf_op jit(solution)/shard_map/ppermute | solution.py:123
  51.8 0.0 collective-permute-done.7.refs_1_
  51.8 1.5 %collective-permute-start.9 = (bf16[4,128,256]{2,1,0:T(8,128)(2,1)S(1)}, bf16[4,128,256]{2,1,0:T(8,128)(2,1)S(1)}, u32[]{:S(2)}, u32[]{:S(2)}) collective-permute-start(bf16[4,128,256]{2,1,0:T(8,128)(2,1)S(1)} %collective-permute-done.7.refs_1_), channel_id=1, source_target_pairs={{2,3},{6,7},{10,11},{14,15},{18,19},{22,23},{26,27},{30,31}} | collective-permute-start | bytes 786440 | tf_op jit(solution)/shard_map/ppermute | solution.py:123
  53.3 0.1 broadcast_in_dim.2.weight_ref
  53.3 0.0 copy-done.1
  53.4 2.5 %shard_map.37.refs_6_ = f32[4,1,9,128,256]{4,3,2,1,0:T(8,128)} custom-call(s32[1,9]{1,0:T(1,128)S(1)} %copy-done.2, bf16[4,128,256]{2,1,0:T(8,128)(2,1)S(1)} %copy-done.1, bf16[4,128,256]{2,1,0:T(8,128)(2,1)S(1)} %copy-done, f32[128,128]{1,0:T(8,128)S(1)} %broadcast_in_dim.2.weight_ref, bf16[4,128,256]{2,1,0:T(8,128)(2,1)S(1)} %copy-done.1, ...), custom_call_target="tpu_custom_call" | custom-call | flops 536870912 | bytes 2097152 | tf_op jit(solution)/shard_map/pallas_call | solution.py:89
  55.9 2.7 %shard_map.38.refs_10_ = f32[4,1,9,128,256]{4,3,2,1,0:T(8,128)} custom-call(s32[1,9]{1,0:T(1,128)S(1)} %copy-done.2, bf16[4,128,256]{2,1,0:T(8,128)(2,1)S(1)} %copy-done.1, bf16[4,128,256]{2,1,0:T(8,128)(2,1)S(1)} %copy-done, f32[128,128]{1,0:T(8,128)S(1)} %broadcast_in_dim.2.weight_ref, ...), custom_call_target="tpu_custom_call", output_to_operand_aliasing={{}: (10, {})} | custom-call | flops 402653184 | bytes 1572864 | tf_op jit(solution)/shard_map/pallas_call | solution.py:89
  58.6 0.0 collective-permute-done.16.refs_6_
  58.6 0.0 collective-permute-done.13.refs_5_
  58.7 0.0 collective-permute-done.9.refs_4_
  58.7 0.0 collective-permute-done.18.refs_8_.refs_9_
  58.7 2.8 %shard_map.39 = f32[4,1,9,128,256]{4,3,2,1,0:T(8,128)} custom-call(s32[1,9]{1,0:T(1,128)S(1)} %copy-done.2, bf16[4,128,256]{2,1,0:T(8,128)(2,1)S(1)} %copy-done.1, bf16[4,128,256]{2,1,0:T(8,128)(2,1)S(1)} %copy-done, f32[128,128]{1,0:T(8,128)S(1)} %broadcast_in_dim.2.weight_ref, ...), custom_call_target="tpu_custom_call", output_to_operand_aliasing={{}: (14, {})} | custom-call | flops 671088640 | bytes 2621440 | tf_op jit(solution)/shard_map/pallas_call | solution.py:89
  (14 shorter events, 0.2 us)
Async XLA Ops:
  0.0 53.3 %copy-start.1 = (bf16[4,128,256]{2,1,0:T(8,128)(2,1)S(1)}, bf16[4,128,256]{2,1,0:T(8,128)(2,1)}, u32[]{:S(2)}) copy-start(bf16[4,128,256]{2,1,0:T(8,128)(2,1)} %re_ref.5) | copy-start | bytes 786436
  0.0 53.3 %copy-start = (bf16[4,128,256]{2,1,0:T(8,128)(2,1)S(1)}, bf16[4,128,256]{2,1,0:T(8,128)(2,1)}, u32[]{:S(2)}) copy-start(bf16[4,128,256]{2,1,0:T(8,128)(2,1)} %im_ref.5) | copy-start | bytes 786436
  0.0 53.4 %copy-start.2 = (s32[1,9]{1,0:T(1,128)S(1)}, s32[1,9]{1,0:T(1,128)}, u32[]{:S(2)}) copy-start(s32[1,9]{1,0:T(1,128)} %offsets_ref.5) | copy-start | bytes 112
  1.3 3.7 %collective-permute-start = (f32[128]{0:T(128)S(1)}, f32[128]{0:T(128)S(1)}, u32[]{:S(2)}, u32[]{:S(2)}) collective-permute-start(f32[128]{0:T(128)S(1)} %add_reduce_fusion), channel_id=1, source_target_pairs={{0,16},{16,0},{1,17},{17,1},{2,18},{18,2},{3,19},{19,3},{4,20},{20... | collective-permute-start | bytes 1544 | tf_op jit(solution)/shard_map/ppermute | solution.py:142
  1.4 10.7 %collective-permute-start.1 = (bf16[4,128,256]{2,1,0:T(8,128)(2,1)}, bf16[4,128,256]{2,1,0:T(8,128)(2,1)S(1)}, u32[]{:S(2)}, u32[]{:S(2)}) collective-permute-start(bf16[4,128,256]{2,1,0:T(8,128)(2,1)} %re_ref.5), channel_id=1, source_target_pairs={{0,12},{1,13},{2,14},{3,15},{4,0},{5,1},{6,2},{7,3},{8,4},{9,5},{1... | collective-permute-start | bytes 786440 | tf_op jit(solution)/shard_map/ppermute | solution.py:123
  6.0 13.5 %collective-permute-start.10 = (bf16[528,256]{1,0:T(8,128)(2,1)S(1)}, bf16[528,256]{1,0:T(8,128)(2,1)S(1)}, u32[]{:S(2)}, u32[]{:S(2)}) collective-permute-start(bf16[528,256]{1,0:T(8,128)(2,1)S(1)} %pad_maximum_fusion.refs_4_), channel_id=1, source_target_pairs={{0,12},{1,13},{2,14},{3,15},{4,0},{5,1},{6,2},{7,3},{8,4},{9,5},{1... | collective-permute-start | bytes 811016 | tf_op jit(solution)/shard_map/ppermute | solution.py:123
  7.2 11.0 %collective-permute-start.3 = (bf16[4,128,256]{2,1,0:T(8,128)(2,1)}, bf16[4,128,256]{2,1,0:T(8,128)(2,1)S(1)}, u32[]{:S(2)}, u32[]{:S(2)}) collective-permute-start(bf16[4,128,256]{2,1,0:T(8,128)(2,1)} %re_ref.5), channel_id=1, source_target_pairs={{2,0},{3,1},{6,4},{7,5},{10,8},{11,9},{14,12},{15,13},{18,16},{19,... | collective-permute-start | bytes 786440 | tf_op jit(solution)/shard_map/ppermute | solution.py:123
  12.0 10.2 %collective-permute-start.2 = (bf16[4,128,256]{2,1,0:T(8,128)(2,1)S(1)}, bf16[4,128,256]{2,1,0:T(8,128)(2,1)S(1)}, u32[]{:S(2)}, u32[]{:S(2)}) collective-permute-start(bf16[4,128,256]{2,1,0:T(8,128)(2,1)S(1)} %collective-permute-done.1.refs_1_), channel_id=1, source_target_pairs={{0,2},{1,3},{2,0},{3,1},{4,6},{5,7},{6,4},{7,5},{8,10},{9,11},{10,... | collective-permute-start | bytes 786440 | tf_op jit(solution)/shard_map/ppermute | solution.py:123
  12.5 11.0 %collective-permute-start.5 = (bf16[4,128,256]{2,1,0:T(8,128)(2,1)S(1)}, bf16[4,128,256]{2,1,0:T(8,128)(2,1)S(1)}, u32[]{:S(2)}, u32[]{:S(2)}) collective-permute-start(bf16[4,128,256]{2,1,0:T(8,128)(2,1)S(1)} %collective-permute-done.1.refs_1_), channel_id=1, source_target_pairs={{0,1},{1,0},{2,3},{3,2},{4,5},{5,4},{6,7},{7,6},{8,9},{9,8},{10,11... | collective-permute-start | bytes 786440 | tf_op jit(solution)/shard_map/ppermute | solution.py:123
  14.0 11.9 %collective-permute-start.6 = (bf16[4,128,256]{2,1,0:T(8,128)(2,1)S(1)}, bf16[4,128,256]{2,1,0:T(8,128)(2,1)S(1)}, u32[]{:S(2)}, u32[]{:S(2)}) collective-permute-start(bf16[4,128,256]{2,1,0:T(8,128)(2,1)S(1)} %collective-permute-done.1.refs_1_), channel_id=1, source_target_pairs={{0,12},{1,13},{2,14},{3,15},{4,0},{5,1},{6,2},{7,3},{8,4},{9,5},{1... | collective-permute-start | bytes 786440 | tf_op jit(solution)/shard_map/ppermute | solution.py:123
  18.2 22.3 %collective-permute-start.19 = (bf16[4,128,256]{2,1,0:T(8,128)(2,1)}, bf16[4,128,256]{2,1,0:T(8,128)(2,1)S(1)}, u32[]{:S(2)}, u32[]{:S(2)}) collective-permute-start(bf16[4,128,256]{2,1,0:T(8,128)(2,1)} %re_ref.5), channel_id=1, source_target_pairs={{1,0},{3,2},{5,4},{7,6},{9,8},{11,10},{13,12},{15,14},{17,16},{19,... | collective-permute-start | bytes 786440 | tf_op jit(solution)/shard_map/ppermute | solution.py:123
  19.5 13.1 %collective-permute-start.14 = (bf16[528,256]{1,0:T(8,128)(2,1)S(1)}, bf16[528,256]{1,0:T(8,128)(2,1)S(1)}, u32[]{:S(2)}, u32[]{:S(2)}) collective-permute-start(bf16[528,256]{1,0:T(8,128)(2,1)S(1)} %collective-permute-done.10.refs_5_), channel_id=1, source_target_pairs={{0,1},{1,0},{2,3},{3,2},{4,5},{5,4},{6,7},{7,6},{8,9},{9,8},{10,11... | collective-permute-start | bytes 811016 | tf_op jit(solution)/shard_map/ppermute | solution.py:123
  22.2 10.3 %collective-permute-start.15 = (bf16[528,256]{1,0:T(8,128)(2,1)S(1)}, bf16[528,256]{1,0:T(8,128)(2,1)S(1)}, u32[]{:S(2)}, u32[]{:S(2)}) collective-permute-start(bf16[528,256]{1,0:T(8,128)(2,1)S(1)} %collective-permute-done.10.refs_5_), channel_id=1, source_target_pairs={{0,12},{1,13},{2,14},{3,15},{4,0},{5,1},{6,2},{7,3},{8,4},{9,5},{1... | collective-permute-start | bytes 811016 | tf_op jit(solution)/shard_map/ppermute | solution.py:123
  23.5 9.8 %collective-permute-start.12 = (bf16[528,256]{1,0:T(8,128)(2,1)S(1)}, bf16[528,256]{1,0:T(8,128)(2,1)S(1)}, u32[]{:S(2)}, u32[]{:S(2)}) collective-permute-start(bf16[528,256]{1,0:T(8,128)(2,1)S(1)} %pad_maximum_fusion.refs_4_), channel_id=1, source_target_pairs={{2,0},{3,1},{6,4},{7,5},{10,8},{11,9},{14,12},{15,13},{18,16},{19,... | collective-permute-start | bytes 811016 | tf_op jit(solution)/shard_map/ppermute | solution.py:123
  26.0 10.2 %collective-permute-start.11 = (bf16[528,256]{1,0:T(8,128)(2,1)S(1)}, bf16[528,256]{1,0:T(8,128)(2,1)S(1)}, u32[]{:S(2)}, u32[]{:S(2)}) collective-permute-start(bf16[528,256]{1,0:T(8,128)(2,1)S(1)} %collective-permute-done.10.refs_5_), channel_id=1, source_target_pairs={{0,2},{1,3},{2,0},{3,1},{4,6},{5,7},{6,4},{7,5},{8,10},{9,11},{10,... | collective-permute-start | bytes 811016 | tf_op jit(solution)/shard_map/ppermute | solution.py:123
  32.6 7.4 %collective-permute-start.4 = (bf16[4,128,256]{2,1,0:T(8,128)(2,1)S(1)}, bf16[4,128,256]{2,1,0:T(8,128)(2,1)S(1)}, u32[]{:S(2)}, u32[]{:S(2)}) collective-permute-start(bf16[4,128,256]{2,1,0:T(8,128)(2,1)S(1)} %broadcast_select_fusion.4), channel_id=1, source_target_pairs={{0,1},{1,0},{2,3},{3,2},{4,5},{5,4},{6,7},{7,6},{8,9},{9,8},{10,11... | collective-permute-start | bytes 786440 | tf_op jit(solution)/shard_map/ppermute | solution.py:123
  32.6 10.3 %collective-permute-start.17 = (bf16[528,256]{1,0:T(8,128)(2,1)S(1)}, bf16[528,256]{1,0:T(8,128)(2,1)S(1)}, u32[]{:S(2)}, u32[]{:S(2)}) collective-permute-start(bf16[528,256]{1,0:T(8,128)(2,1)S(1)} %collective-permute-done.14.refs_3_), channel_id=1, source_target_pairs={{0,12},{1,13},{3,15},{4,0},{5,1},{7,3},{8,4},{9,5},{11,7},{12,8},{... | collective-permute-start | bytes 811016 | tf_op jit(solution)/shard_map/ppermute | solution.py:123
  33.3 14.3 %collective-permute-start.20 = (bf16[528,256]{1,0:T(8,128)(2,1)S(1)}, bf16[528,256]{1,0:T(8,128)(2,1)S(1)}, u32[]{:S(2)}, u32[]{:S(2)}) collective-permute-start(bf16[528,256]{1,0:T(8,128)(2,1)S(1)} %pad_maximum_fusion.refs_4_), channel_id=1, source_target_pairs={{1,0},{3,2},{5,4},{7,6},{9,8},{11,10},{13,12},{15,14},{17,16},{19,... | collective-permute-start | bytes 811016 | tf_op jit(solution)/shard_map/ppermute | solution.py:123
  36.2 15.6 %collective-permute-start.7 = (bf16[4,128,256]{2,1,0:T(8,128)(2,1)S(1)}, bf16[4,128,256]{2,1,0:T(8,128)(2,1)S(1)}, u32[]{:S(2)}, u32[]{:S(2)}) collective-permute-start(bf16[4,128,256]{2,1,0:T(8,128)(2,1)S(1)} %broadcast_select_fusion.3), channel_id=1, source_target_pairs={{0,2},{1,3},{2,0},{3,1},{4,6},{5,7},{6,4},{7,5},{8,10},{9,11},{10,... | collective-permute-start | bytes 786440 | tf_op jit(solution)/shard_map/ppermute | solution.py:123
  40.0 18.6 %collective-permute-start.16 = (bf16[528,256]{1,0:T(8,128)(2,1)S(1)}, bf16[528,256]{1,0:T(8,128)(2,1)S(1)}, u32[]{:S(2)}, u32[]{:S(2)}) collective-permute-start(bf16[528,256]{1,0:T(8,128)(2,1)S(1)} %broadcast_select_fusion), channel_id=1, source_target_pairs={{0,2},{1,3},{2,0},{3,1},{4,6},{5,7},{6,4},{7,5},{8,10},{9,11},{10,... | collective-permute-start | bytes 811016 | tf_op jit(solution)/shard_map/ppermute | solution.py:123
  40.5 18.2 %collective-permute-start.13 = (bf16[528,256]{1,0:T(8,128)(2,1)S(1)}, bf16[528,256]{1,0:T(8,128)(2,1)S(1)}, u32[]{:S(2)}, u32[]{:S(2)}) collective-permute-start(bf16[528,256]{1,0:T(8,128)(2,1)S(1)} %broadcast_select_fusion.1), channel_id=1, source_target_pairs={{0,1},{1,0},{2,3},{3,2},{4,5},{5,4},{6,7},{7,6},{8,9},{9,8},{10,11... | collective-permute-start | bytes 811016 | tf_op jit(solution)/shard_map/ppermute | solution.py:123
  42.8 15.9 %collective-permute-start.18 = (bf16[528,256]{1,0:T(8,128)(2,1)S(1)}, bf16[528,256]{1,0:T(8,128)(2,1)S(1)}, u32[]{:S(2)}, u32[]{:S(2)}) collective-permute-start(bf16[528,256]{1,0:T(8,128)(2,1)S(1)} %collective-permute-done.17.refs_7_), channel_id=1, source_target_pairs={{0,2},{1,3},{4,6},{5,7},{8,10},{9,11},{12,14},{13,15},{16,18},{17,... | collective-permute-start | bytes 811016 | tf_op jit(solution)/shard_map/ppermute | solution.py:123
  47.6 11.0 %collective-permute-start.8 = (bf16[4,128,256]{2,1,0:T(8,128)(2,1)S(1)}, bf16[4,128,256]{2,1,0:T(8,128)(2,1)S(1)}, u32[]{:S(2)}, u32[]{:S(2)}) collective-permute-start(bf16[4,128,256]{2,1,0:T(8,128)(2,1)S(1)} %broadcast_select_fusion.2), channel_id=1, source_target_pairs={{1,13},{2,14},{3,15},{5,1},{6,2},{7,3},{9,5},{10,6},{11,7},{13,9},... | collective-permute-start | bytes 786440 | tf_op jit(solution)/shard_map/ppermute | solution.py:123
  51.8 6.9 %collective-permute-start.9 = (bf16[4,128,256]{2,1,0:T(8,128)(2,1)S(1)}, bf16[4,128,256]{2,1,0:T(8,128)(2,1)S(1)}, u32[]{:S(2)}, u32[]{:S(2)}) collective-permute-start(bf16[4,128,256]{2,1,0:T(8,128)(2,1)S(1)} %collective-permute-done.7.refs_1_), channel_id=1, source_target_pairs={{2,3},{6,7},{10,11},{14,15},{18,19},{22,23},{26,27},{30,31}} | collective-permute-start | bytes 786440 | tf_op jit(solution)/shard_map/ppermute | solution.py:123
where the time goes:
time: 61.8 us; the launch traced here: 61.5 us
  starting transfers between devices  36.7 us (59%)
  waiting for transfers between devices  14 us (23%)
  Pallas kernels  8.06 us (13%)
  other arithmetic  2.44 us (4%)
    ppermute x20, starting transfers between devices, send(): return lax.ppermute(value, BLOCKS, links)  36.6 us
    ppermute x20, waiting for transfers between devices, send(): return lax.ppermute(value, BLOCKS, links)  14 us
    pallas_call x3, Pallas kernels, products(): pl.pallas_call(functools.partial(product_kernel, [entry for _, entry in g...  8.06 us
    reduce_sum x1, other arithmetic, local(): power_half = jnp.sum(re32 * re32 + im32 * im32, axis=(0, 2))  1.27 us
  transfers between devices with their start and end apart: 21, of which 4 were waited for; matrix products, arithmetic and copies ran while one was open for 2% of the time, Pallas kernels for 9%

commit v1 on v0

v1 whole, which is shorter than its diff:
```python
import functools
import math

import jax
import jax.numpy as jnp
from jax import lax
from jax.experimental import pallas as pl
from jax.experimental.pallas import tpu as pltpu
from jax.sharding import PartitionSpec as P


BLOCKS = ("sr", "sc")
GAIN_PARTS = 3
GAIN_ROWS = 16
VMEM_BYTES = 16 << 20
CHUNK = 8


def vmem():
    return pl.BlockSpec(memory_space=pltpu.VMEM)


def params():
    return pltpu.CompilerParams(vmem_limit_bytes=VMEM_BYTES)


def power_kernel(re_ref, im_ref, re_out, im_out, sum_ref, sems):
    size = re_ref.shape[0]
    rows = sum_ref.shape[1]
    halves = (re_out, im_out.at[pl.ds(0, size)])
    copies = [
        pltpu.make_async_copy(source, half, sems.at[i])
        for i, (source, half) in enumerate(zip((re_ref, im_ref), halves))
    ]
    for copy in copies:
        copy.start()
    im_out[size:] = jnp.zeros((GAIN_ROWS, im_out.shape[1]), im_out.dtype)
    total = None
    for copy, half in zip(copies, halves):
        copy.wait()
        for f in range(size // rows):
            piece = half[f * rows : (f + 1) * rows, :].astype(jnp.float32)
            total = piece * piece if total is None else total + piece * piece
    folded = total[:, :rows]
    for start in range(rows, total.shape[1], rows):
        folded = folded + total[:, start : start + rows]
    sum_ref[...] = jnp.broadcast_to(jnp.sum(folded.T, axis=0, keepdims=True), sum_ref.shape)


def cat_kernel(samples, norm, im_ref, mine_ref, other_ref, out_ref, weight_ref):
    size = im_ref.shape[0] - GAIN_ROWS
    rows = mine_ref.shape[1]
    gain = lax.rsqrt((mine_ref[0:1] + other_ref[0:1]) / samples)
    weight_ref[...] = jnp.broadcast_to(gain * norm, (rows, rows)).T
    parts, rest = [], gain
    for _ in range(GAIN_PARTS):
        part = rest.astype(jnp.bfloat16).astype(jnp.float32)
        parts.append(part)
        rest = rest - part
    parts.append(jnp.zeros((GAIN_ROWS - GAIN_PARTS, rows), jnp.float32))
    tail = jnp.concatenate(parts, axis=0)
    out_ref[size:, :rows] = tail.astype(jnp.bfloat16)


def product_kernel(entries, offsets_ref, re_ref, im_ref, weight_ref, *refs):
    pair_count = len(entries)
    reals = refs[:pair_count]
    imags = refs[pair_count : 2 * pair_count]
    out_ref, stage, sems = refs[-3:]
    _, bins, rows, _ = stage.shape
    slot_count = offsets_ref.shape[1]
    contract = (((1,), (1,)), ((), ()))
    column = lax.axis_index("sc")

    wanted, slots = [], []
    for entry in entries:
        offset, use = entry(column)
        use = jnp.logical_and(use, jnp.logical_and(offset >= 0, offset < slot_count))

        def find(m, found, offset=offset):
            return jnp.where(offsets_ref[0, m] == offset, m, found)

        wanted.append(use)
        slots.append(lax.fori_loop(0, slot_count, find, jnp.int32(0), unroll=True))

    def copy_out(i, f):
        return pltpu.make_async_copy(
            stage.at[i, f], out_ref.at[f, 0, slots[i]], sems.at[i, f]
        )

    for i in range(pair_count):

        @pl.when(wanted[i])
        def _(i=i):
            parts = imags[i][pl.ds(bins * rows, GAIN_ROWS), :rows].astype(jnp.float32)
            gain = parts[0:1] + parts[1:2] + parts[2:3]
            weight = weight_ref[...] * gain
            for f in range(bins):
                low = pl.ds(f * rows, rows)
                own = jnp.concatenate([re_ref[low, :], im_ref[low, :]], axis=0)
                other = jnp.concatenate([reals[i][low, :], imags[i][low, :]], axis=0)
                four = lax.dot_general(
                    own, other, contract, preferred_element_type=jnp.float32
                )
                real = four[:rows, :rows] + four[rows:, rows:]
                imag = four[rows:, :rows] - four[:rows, rows:]
                stage[i, f, :, :rows] = real * weight
                stage[i, f, :, rows:] = imag * weight
                copy_out(i, f).start()

    for i in range(pair_count):

        @pl.when(wanted[i])
        def _(i=i):
            for f in range(bins):
                copy_out(i, f).wait()


def products(offsets, own, weight, group, out_shape, out):
    bins, _, _, rows, _ = out_shape.shape
    segs = own[0].shape[1]
    count = len(group)
    args = [offsets, *own, weight]
    args += [pair[0] for pair, _ in group] + [pair[1] for pair, _ in group]
    specs = [pl.BlockSpec(memory_space=pltpu.SMEM)] + [vmem()] * (len(args) - 1)
    aliases = {}
    if out is not None:
        aliases = {len(args): 0}
        args.append(out)
        specs.append(pl.BlockSpec(memory_space=pl.ANY))
    return pl.pallas_call(
        functools.partial(product_kernel, [entry for _, entry in group]),
        out_shape=out_shape,
        in_specs=specs,
        out_specs=pl.BlockSpec(memory_space=pl.ANY),
        scratch_shapes=[
            pltpu.VMEM((count, bins, rows, 2 * rows), jnp.float32),
            pltpu.SemaphoreType.DMA((count, bins)),
        ],
        input_output_aliases=aliases,
        compiler_params=params(),
        cost_estimate=pl.CostEstimate(
            flops=count * bins * 8 * rows * rows * segs,
            bytes_accessed=count * bins * rows * 2 * rows * 4,
            transcendentals=0,
        ),
    )(*args)


def local(sr, sc, spec_re, spec_im, offsets):
    bins, rows, segs = spec_re.shape
    size = bins * rows
    slot_count = offsets.shape[1]
    half = sr // 2
    samples = float(bins * lax.axis_size("fr") * segs)
    norm = 1.0 / math.sqrt(segs)
    column = lax.axis_index("sc")
    is_upper = (column & 2) != 0
    everyone = range(sc)
    upper = [s for s in everyone if s & 2]
    lower = [s for s in everyone if not s & 2]
    odd = [s for s in everyone if s & 1]

    def send(value, route):
        links = []
        for z in range(sr):
            for s in everyone:
                target = route(z, s)
                if target is not None:
                    links.append((z * sc + s, (target[0] % sr) * sc + target[1]))
        return lax.ppermute(value, BLOCKS, links)

    def both(pair, route):
        return send(pair[0], route), send(pair[1], route)

    def down(columns=everyone):
        return lambda z, s: (z - 1, s) if s in columns else None

    def flip(bit, columns=everyone):
        return lambda z, s: (z, s ^ bit) if s in columns else None

    flat_re = spec_re.reshape(size, segs)
    flat_im = spec_im.reshape(size, segs)
    tall = jax.ShapeDtypeStruct((size + GAIN_ROWS, segs), spec_im.dtype)
    anywhere = pl.BlockSpec(memory_space=pltpu.HBM)
    own_re, bare, mine = pl.pallas_call(
        power_kernel,
        out_shape=(
            jax.ShapeDtypeStruct((size, segs), spec_re.dtype),
            tall,
            jax.ShapeDtypeStruct((8, rows), jnp.float32),
        ),
        in_specs=[anywhere] * 2,
        out_specs=(vmem(),) * 3,
        scratch_shapes=[pltpu.SemaphoreType.DMA((2,))],
        compiler_params=params(),
        cost_estimate=pl.CostEstimate(
            flops=4 * size * segs, bytes_accessed=4 * size * segs, transcendentals=0
        ),
        name="power",
    )(flat_re, flat_im)
    other = lax.ppermute(mine, "fr", [(0, 1), (1, 0)])
    own_tail, weight = pl.pallas_call(
        functools.partial(cat_kernel, samples, norm),
        out_shape=(tall, jax.ShapeDtypeStruct((rows, rows), jnp.float32)),
        in_specs=[vmem()] * 3,
        out_specs=(vmem(), vmem()),
        input_output_aliases={0: 0},
        compiler_params=params(),
        cost_estimate=pl.CostEstimate(
            flops=rows * rows, bytes_accessed=4 * rows * rows, transcendentals=rows
        ),
        name="cat",
    )(bare, mine, other)
    own = (own_re, own_tail)

    planes = [own, (send(flat_re, down()), send(own_tail, down()))]
    for _ in range(1, half):
        planes.append(both(planes[-1], down()))
    near, far = planes[half - 1], planes[half]
    v1, v2 = both(own, flip(2, upper)), both(near, flip(2))
    u1a, u2 = send(own_re, flip(1, odd)), both(near, flip(1))

    y3 = tuple(send(jnp.where(is_upper, u2[h], far[h]), flip(2)) for h in range(2))
    x3 = tuple(send(jnp.where(is_upper, v2[h], v1[h]), flip(1)) for h in range(2))
    z3b = send(u2[1], down([0, 1, 3]))
    late, soon = lax.optimization_barrier((x3[0], u2[0]))
    z3a = send(jnp.where(column == 2, late, soon), down([1, 2, 3]))
    wide = jnp.pad(y3[0], ((0, GAIN_ROWS), (0, 0)))
    xl = send(jnp.where((column & 1) == 1, own_tail, wide), flip(1, [1, 2, 3]))
    yfb = send(z3b, flip(2, lower))

    def entry(plane, bit, use=lambda column: True):
        return lambda column: (plane * sc + (column ^ bit) - column, use(column))

    def x3_entry(column):
        plane = jnp.where((column & 2) != 0, half - 1, 0)
        return plane * sc + (column ^ 3) - column, True

    def y3_entry(column):
        is_upper = (column & 2) != 0
        plane = jnp.where(is_upper, half, half - 1)
        return plane * sc + (column ^ jnp.where(is_upper, 2, 3)) - column, True

    soon_group = [
        (own, entry(0, 0)),
        (near, entry(half - 1, 0)),
        (v1, entry(0, 2)),
        (u2, entry(half - 1, 1)),
        (v2, entry(half - 1, 2)),
        (far, entry(half, 0)),
    ]
    for j in range(1, half - 1):
        u = both(planes[j], flip(1))
        v = both(planes[j], flip(2))
        d = both(v, flip(1))
        soon_group += [(p, entry(j, bit)) for bit, p in enumerate((planes[j], u, v, d))]
    groups = [soon_group[i : i + CHUNK] for i in range(0, len(soon_group), CHUNK)]
    groups.append(
        [
            (x3, x3_entry),
            (y3, y3_entry),
            ((u1a, xl), entry(0, 1)),
            ((z3a, z3b), entry(half, 1, lambda column: (column & 1) == 1)),
            ((z3a, yfb), entry(half, 3, lambda column: column == 2)),
            ((xl, yfb), entry(half, 3, lambda column: column == 3)),
        ]
    )
    out_shape = jax.ShapeDtypeStruct((bins, 1, slot_count, rows, 2 * rows), jnp.float32)
    out = None
    for group in groups:
        out = products(offsets, own, weight, group, out_shape, out)
    return out


def solution(mesh):
    sr, sc = mesh.shape["sr"], mesh.shape["sc"]
    placed = (P("fr", ("sr", "sc"), None), P("fr", ("sr", "sc"), None), P(("sr", "sc"), None))

    def body(*args):
        return local(sr, sc, *args)

    return jax.shard_map(
        body,
        mesh=mesh,
        in_specs=placed,
        out_specs=P("fr", ("sr", "sc"), None, None, None),
        check_vma=False,
    )
```

time: 61.8 us -> 65 us (1.052)
  the two profiles are of different devices: /device:TPU:4 before, /device:TPU:2 now
where the time goes in v1:
time: 65 us; the launch traced here: 64.7 us
  starting transfers between devices  35.7 us (55%)
  waiting for transfers between devices  20.4 us (31%)
  Pallas kernels  6.25 us (10%)
  local copies, waits for them, and re-layouts  1.9 us (3%)
    ppermute x19, starting transfers between devices, send(): return lax.ppermute(value, BLOCKS, links)  35.7 us
    ppermute x19, waiting for transfers between devices, send(): return lax.ppermute(value, BLOCKS, links)  19.2 us
    pallas_call x2, Pallas kernels, products(): pl.pallas_call(functools.partial(product_kernel, [entry for _, entry in g...  5.92 us
    unnamed x6, local copies, waits for them, and re-layouts  1.9 us
  transfers between devices with their start and end apart: 20, of which 9 were waited for; matrix products, arithmetic and copies ran while one was open for 0% of the time, Pallas kernels for 6%

profile of v1, /device:TPU:2, one launch (start us, length us, event | category | flops | bytes accessed | tf_op | source)
XLA Modules:
  0.0 64.7 jit_solution(853303089597139907)
XLA Ops:
  0.0 3.6 %collective-permute-start.1 = (bf16[512,256]{1,0:T(8,128)(2,1)}, bf16[512,256]{1,0:T(8,128)(2,1)S(1)}, u32[]{:S(2)}, u32[]{:S(2)}) collective-permute-start(bf16[512,256]{1,0:T(8,128)(2,1)} %bitcast.3), channel_id=1, source_target_pairs={{0,12},{1,13},{2,14},{3,15},{4,0},{5,1},{6,2},{7,3},{8,4},{9,5},{1... | collective-permute-start | bytes 786440 | tf_op jit(solution)/shard_map/ppermute | solution.py:171
  3.6 0.9 %copy-done = bf16[4,128,256]{2,1,0:T(8,128)(2,1)S(1)} copy-done((bf16[4,128,256]{2,1,0:T(8,128)(2,1)S(1)}, bf16[4,128,256]{2,1,0:T(8,128)(2,1)}, u32[]{:S(2)}) %copy-start) | copy-done | bytes 262168
  4.6 0.9 %copy-done.1 = bf16[4,128,256]{2,1,0:T(8,128)(2,1)S(1)} copy-done((bf16[4,128,256]{2,1,0:T(8,128)(2,1)S(1)}, bf16[4,128,256]{2,1,0:T(8,128)(2,1)}, u32[]{:S(2)}) %copy-start.1) | copy-done | bytes 262168
  5.5 0.2 power.1
  5.7 0.1 collective-permute-start
  5.8 1.2 %collective-permute-done.other_ref = f32[8,128]{1,0:T(8,128)S(1)} collective-permute-done((f32[8,128]{1,0:T(8,128)S(1)}, f32[8,128]{1,0:T(8,128)S(1)}, u32[]{:S(2)}, u32[]{:S(2)}) %collective-permute-start) | collective-permute-done | bytes 4128 | tf_op jit(solution)/shard_map/ppermute | solution.py:202
  7.0 0.1 cat.1
  7.1 0.5 collective-permute-start.11
  7.6 3.0 %collective-permute-done.1.refs_1_ = bf16[512,256]{1,0:T(8,128)(2,1)S(1)} collective-permute-done((bf16[512,256]{1,0:T(8,128)(2,1)}, bf16[512,256]{1,0:T(8,128)(2,1)S(1)}, u32[]{:S(2)}, u32[]{:S(2)}) %collective-permute-start.1) | collective-permute-done | bytes 262176 | tf_op jit(solution)/shard_map/ppermute | solution.py:171
  10.6 4.2 %collective-permute-start.6 = (bf16[512,256]{1,0:T(8,128)(2,1)S(1)}, bf16[512,256]{1,0:T(8,128)(2,1)S(1)}, u32[]{:S(2)}, u32[]{:S(2)}) collective-permute-start(bf16[512,256]{1,0:T(8,128)(2,1)S(1)} %collective-permute-done.1.refs_1_), channel_id=1, source_target_pairs={{0,12},{1,13},{2,14},{3,15},{4,0},{5,1},{6,2},{7,3},{8,4},{9,5},{1... | collective-permute-start | bytes 786440 | tf_op jit(solution)/shard_map/ppermute | solution.py:171
  14.8 0.5 collective-permute-start.5
  15.3 1.3 %collective-permute-start.3 = (bf16[512,256]{1,0:T(8,128)(2,1)S(1)}, bf16[512,256]{1,0:T(8,128)(2,1)S(1)}, u32[]{:S(2)}, u32[]{:S(2)}) collective-permute-start(bf16[512,256]{1,0:T(8,128)(2,1)S(1)} %get-tuple-element.12.re_ref.refs_0_), channel_id=1, source_target_pairs={{2,0},{3,1},{6,4},{7,5},{10,8},{11,9},{14,12},{15,13},{18,16},{19,... | collective-permute-start | bytes 786440 | tf_op jit(solution)/shard_map/ppermute | solution.py:171
  16.6 2.7 %collective-permute-start.2 = (bf16[512,256]{1,0:T(8,128)(2,1)S(1)}, bf16[512,256]{1,0:T(8,128)(2,1)S(1)}, u32[]{:S(2)}, u32[]{:S(2)}) collective-permute-start(bf16[512,256]{1,0:T(8,128)(2,1)S(1)} %collective-permute-done.1.refs_1_), channel_id=1, source_target_pairs={{0,2},{1,3},{2,0},{3,1},{4,6},{5,7},{6,4},{7,5},{8,10},{9,11},{10,... | collective-permute-start | bytes 786440 | tf_op jit(solution)/shard_map/ppermute | solution.py:171
  19.3 0.0 collective-permute-done.11.refs_7_
  19.3 3.4 %collective-permute-start.8 = (bf16[512,256]{1,0:T(8,128)(2,1)S(1)}, bf16[512,256]{1,0:T(8,128)(2,1)S(1)}, u32[]{:S(2)}, u32[]{:S(2)}) collective-permute-start(bf16[512,256]{1,0:T(8,128)(2,1)S(1)} %get-tuple-element.12.re_ref.refs_0_), channel_id=1, source_target_pairs={{1,0},{3,2},{5,4},{7,6},{9,8},{11,10},{13,12},{15,14},{17,16},{19,... | collective-permute-start | bytes 786440 | tf_op jit(solution)/shard_map/ppermute | solution.py:171
  22.7 0.0 collective-permute-done.6.refs_5_
  22.8 2.3 %collective-permute-start.16 = (bf16[528,256]{1,0:T(8,128)(2,1)S(1)}, bf16[528,256]{1,0:T(8,128)(2,1)S(1)}, u32[]{:S(2)}, u32[]{:S(2)}) collective-permute-start(bf16[528,256]{1,0:T(8,128)(2,1)S(1)} %collective-permute-done.11.refs_7_), channel_id=1, source_target_pairs={{0,12},{1,13},{2,14},{3,15},{4,0},{5,1},{6,2},{7,3},{8,4},{9,5},{1... | collective-permute-start | bytes 811016 | tf_op jit(solution)/shard_map/ppermute | solution.py:171
  25.1 0.0 collective-permute-done.5.refs_3_
  25.1 0.5 collective-permute-start.15
  25.6 0.0 collective-permute-done.3.refs_2_
  25.7 1.3 %collective-permute-start.13 = (bf16[528,256]{1,0:T(8,128)(2,1)S(1)}, bf16[528,256]{1,0:T(8,128)(2,1)S(1)}, u32[]{:S(2)}, u32[]{:S(2)}) collective-permute-start(bf16[528,256]{1,0:T(8,128)(2,1)S(1)} %get-tuple-element.15.im_ref.refs_6_), channel_id=1, source_target_pairs={{2,0},{3,1},{6,4},{7,5},{10,8},{11,9},{14,12},{15,13},{18,16},{19,... | collective-permute-start | bytes 811016 | tf_op jit(solution)/shard_map/ppermute | solution.py:171
  27.0 1.4 %collective-permute-done.2.refs_4_ = bf16[512,256]{1,0:T(8,128)(2,1)S(1)} collective-permute-done((bf16[512,256]{1,0:T(8,128)(2,1)S(1)}, bf16[512,256]{1,0:T(8,128)(2,1)S(1)}, u32[]{:S(2)}, u32[]{:S(2)}) %collective-permute-start.2) | collective-permute-done | bytes 262176 | tf_op jit(solution)/shard_map/ppermute | solution.py:171
  28.3 1.4 %collective-permute-start.12 = (bf16[528,256]{1,0:T(8,128)(2,1)S(1)}, bf16[528,256]{1,0:T(8,128)(2,1)S(1)}, u32[]{:S(2)}, u32[]{:S(2)}) collective-permute-start(bf16[528,256]{1,0:T(8,128)(2,1)S(1)} %collective-permute-done.11.refs_7_), channel_id=1, source_target_pairs={{0,2},{1,3},{2,0},{3,1},{4,6},{5,7},{6,4},{7,5},{8,10},{9,11},{10,... | collective-permute-start | bytes 811016 | tf_op jit(solution)/shard_map/ppermute | solution.py:171
  29.7 0.2 collective-permute-done.16.refs_11_
  30.0 1.5 %collective-permute-start.7 = (bf16[512,256]{1,0:T(8,128)(2,1)S(1)}, bf16[512,256]{1,0:T(8,128)(2,1)S(1)}, u32[]{:S(2)}, u32[]{:S(2)}) collective-permute-start(bf16[512,256]{1,0:T(8,128)(2,1)S(1)} %broadcast_select_fusion.3), channel_id=1, source_target_pairs={{0,2},{1,3},{2,0},{3,1},{4,6},{5,7},{6,4},{7,5},{8,10},{9,11},{10,... | collective-permute-start | bytes 786440 | tf_op jit(solution)/shard_map/ppermute | solution.py:171
  31.5 0.9 %collective-permute-done.15.refs_9_ = bf16[528,256]{1,0:T(8,128)(2,1)S(1)} collective-permute-done((bf16[528,256]{1,0:T(8,128)(2,1)S(1)}, bf16[528,256]{1,0:T(8,128)(2,1)S(1)}, u32[]{:S(2)}, u32[]{:S(2)}) %collective-permute-start.15) | collective-permute-done | bytes 270368 | tf_op jit(solution)/shard_map/ppermute | solution.py:171
  32.4 2.5 %collective-permute-start.4 = (bf16[512,256]{1,0:T(8,128)(2,1)S(1)}, bf16[512,256]{1,0:T(8,128)(2,1)S(1)}, u32[]{:S(2)}, u32[]{:S(2)}) collective-permute-start(bf16[512,256]{1,0:T(8,128)(2,1)S(1)} %broadcast_select_fusion.4), channel_id=1, source_target_pairs={{0,1},{1,0},{2,3},{3,2},{4,5},{5,4},{6,7},{7,6},{8,9},{9,8},{10,11... | collective-permute-start | bytes 786440 | tf_op jit(solution)/shard_map/ppermute | solution.py:171
  34.9 2.0 %collective-permute-done.13.refs_8_ = bf16[528,256]{1,0:T(8,128)(2,1)S(1)} collective-permute-done((bf16[528,256]{1,0:T(8,128)(2,1)S(1)}, bf16[528,256]{1,0:T(8,128)(2,1)S(1)}, u32[]{:S(2)}, u32[]{:S(2)}) %collective-permute-start.13) | collective-permute-done | bytes 270368 | tf_op jit(solution)/shard_map/ppermute | solution.py:171
  36.9 0.0 collective-permute-start.17
  36.9 5.8 %collective-permute-done.12.refs_10_ = bf16[528,256]{1,0:T(8,128)(2,1)S(1)} collective-permute-done((bf16[528,256]{1,0:T(8,128)(2,1)S(1)}, bf16[528,256]{1,0:T(8,128)(2,1)S(1)}, u32[]{:S(2)}, u32[]{:S(2)}) %collective-permute-start.12) | collective-permute-done | bytes 270368 | tf_op jit(solution)/shard_map/ppermute | solution.py:171
  42.7 2.0 %collective-permute-start.18 = (bf16[528,256]{1,0:T(8,128)(2,1)S(1)}, bf16[528,256]{1,0:T(8,128)(2,1)S(1)}, u32[]{:S(2)}, u32[]{:S(2)}) collective-permute-start(bf16[528,256]{1,0:T(8,128)(2,1)S(1)} %collective-permute-done.15.refs_9_), channel_id=1, source_target_pairs={{0,12},{1,13},{3,15},{4,0},{5,1},{7,3},{8,4},{9,5},{11,7},{12,8},{... | collective-permute-start | bytes 811016 | tf_op jit(solution)/shard_map/ppermute | solution.py:171
  44.8 3.5 %collective-permute-done.7.refs_1_ = bf16[512,256]{1,0:T(8,128)(2,1)S(1)} collective-permute-done((bf16[512,256]{1,0:T(8,128)(2,1)S(1)}, bf16[512,256]{1,0:T(8,128)(2,1)S(1)}, u32[]{:S(2)}, u32[]{:S(2)}) %collective-permute-start.7) | collective-permute-done | bytes 262176 | tf_op jit(solution)/shard_map/ppermute | solution.py:171
  48.3 1.5 %collective-permute-start.14 = (bf16[528,256]{1,0:T(8,128)(2,1)S(1)}, bf16[528,256]{1,0:T(8,128)(2,1)S(1)}, u32[]{:S(2)}, u32[]{:S(2)}) collective-permute-start(bf16[528,256]{1,0:T(8,128)(2,1)S(1)} %broadcast_select_fusion.1), channel_id=1, source_target_pairs={{0,1},{1,0},{2,3},{3,2},{4,5},{5,4},{6,7},{7,6},{8,9},{9,8},{10,11... | collective-permute-start | bytes 811016 | tf_op jit(solution)/shard_map/ppermute | solution.py:171
  49.8 0.1 pad_select_fusion
  49.9 0.0 collective-permute-done.4.refs_0_
  49.9 2.5 %collective-permute-start.10 = (bf16[528,256]{1,0:T(8,128)(2,1)S(1)}, bf16[528,256]{1,0:T(8,128)(2,1)S(1)}, u32[]{:S(2)}, u32[]{:S(2)}) collective-permute-start(bf16[528,256]{1,0:T(8,128)(2,1)S(1)} %pad_select_fusion), channel_id=1, source_target_pairs={{1,0},{2,3},{3,2},{5,4},{6,7},{7,6},{9,8},{10,11},{11,10},{13,12},... | collective-permute-start | bytes 811016 | tf_op jit(solution)/shard_map/ppermute | solution.py:171
  52.3 0.0 collective-permute-done.18.refs_9_
  52.4 1.5 %collective-permute-start.19 = (bf16[528,256]{1,0:T(8,128)(2,1)S(1)}, bf16[528,256]{1,0:T(8,128)(2,1)S(1)}, u32[]{:S(2)}, u32[]{:S(2)}) collective-permute-start(bf16[528,256]{1,0:T(8,128)(2,1)S(1)} %collective-permute-done.18.refs_9_), channel_id=1, source_target_pairs={{0,2},{1,3},{4,6},{5,7},{8,10},{9,11},{12,14},{13,15},{16,18},{17,... | collective-permute-start | bytes 811016 | tf_op jit(solution)/shard_map/ppermute | solution.py:171
  53.9 0.0 collective-permute-done.8.refs_2_
  53.9 2.5 %collective-permute-start.9 = (bf16[512,256]{1,0:T(8,128)(2,1)S(1)}, bf16[512,256]{1,0:T(8,128)(2,1)S(1)}, u32[]{:S(2)}, u32[]{:S(2)}) collective-permute-start(bf16[512,256]{1,0:T(8,128)(2,1)S(1)} %broadcast_select_fusion.2), channel_id=1, source_target_pairs={{1,13},{2,14},{3,15},{5,1},{6,2},{7,3},{9,5},{10,6},{11,7},{13,9},... | collective-permute-start | bytes 786440 | tf_op jit(solution)/shard_map/ppermute | solution.py:171
  56.4 0.0 copy-done.2
  56.4 3.4 %shard_map.37.refs_12_ = f32[4,1,9,128,256]{4,3,2,1,0:T(8,128)} custom-call(s32[1,9]{1,0:T(1,128)S(1)} %copy-done.2, bf16[512,256]{1,0:T(8,128)(2,1)S(1)} %get-tuple-element.12.re_ref.refs_0_, bf16[528,256]{1,0:T(8,128)(2,1)S(1)} %get-tuple-element.15.im_ref.refs_6_, f32[128,128]{1,0:T(8,128)S(1)} %get-tuple-element.16.weight_ref, ...), custom_call_target="tpu_custom_call" | custom-call | flops 805306368 | bytes 3145728 | tf_op jit(solution)/shard_map/pallas_call | solution.py:131
  59.8 0.0 collective-permute-done.17.refs_7_
  59.8 0.0 collective-permute-done.14.refs_6_
  59.8 2.3 %collective-permute-done.9.refs_3_.refs_4_ = bf16[512,256]{1,0:T(8,128)(2,1)S(1)} collective-permute-done((bf16[512,256]{1,0:T(8,128)(2,1)S(1)}, bf16[512,256]{1,0:T(8,128)(2,1)S(1)}, u32[]{:S(2)}, u32[]{:S(2)}) %collective-permute-start.9) | collective-permute-done | bytes 262176 | tf_op jit(solution)/shard_map/ppermute | solution.py:171
  62.1 0.0 collective-permute-done.10.refs_5_.refs_8_
  62.1 0.0 collective-permute-done.19.refs_10_.refs_11_
  62.1 2.6 %shard_map.38 = f32[4,1,9,128,256]{4,3,2,1,0:T(8,128)} custom-call(s32[1,9]{1,0:T(1,128)S(1)} %copy-done.2, bf16[512,256]{1,0:T(8,128)(2,1)S(1)} %get-tuple-element.12.re_ref.refs_0_, bf16[528,256]{1,0:T(8,128)(2,1)S(1)} %get-tuple-element.15.im_ref.refs_6_, f32[128,128]{1,0:T(8,128)S(1)} %get-tuple-element.16.weight_ref, ...), custom_call_target="tpu_custom_call", output_to_operand_aliasing={{}: (16, {})} | custom-call | flops 805306368 | bytes 3145728 | tf_op jit(solution)/shard_map/pallas_call | solution.py:131
  (8 shorter events, 0.2 us)
Async XLA Ops:
  0.0 56.4 %copy-start.2 = (s32[1,9]{1,0:T(1,128)S(1)}, s32[1,9]{1,0:T(1,128)}, u32[]{:S(2)}) copy-start(s32[1,9]{1,0:T(1,128)} %offsets_ref.3) | copy-start | bytes 112
  0.0 10.6 %collective-permute-start.1 = (bf16[512,256]{1,0:T(8,128)(2,1)}, bf16[512,256]{1,0:T(8,128)(2,1)S(1)}, u32[]{:S(2)}, u32[]{:S(2)}) collective-permute-start(bf16[512,256]{1,0:T(8,128)(2,1)} %bitcast.3), channel_id=1, source_target_pairs={{0,12},{1,13},{2,14},{3,15},{4,0},{5,1},{6,2},{7,3},{8,4},{9,5},{1... | collective-permute-start | bytes 786440 | tf_op jit(solution)/shard_map/ppermute | solution.py:171
  3.6 0.9 %copy-start = (bf16[4,128,256]{2,1,0:T(8,128)(2,1)S(1)}, bf16[4,128,256]{2,1,0:T(8,128)(2,1)}, u32[]{:S(2)}) copy-start(bf16[4,128,256]{2,1,0:T(8,128)(2,1)} %param.4) | copy-start | bytes 786436
  4.6 0.9 %copy-start.1 = (bf16[4,128,256]{2,1,0:T(8,128)(2,1)S(1)}, bf16[4,128,256]{2,1,0:T(8,128)(2,1)}, u32[]{:S(2)}) copy-start(bf16[4,128,256]{2,1,0:T(8,128)(2,1)} %param.3) | copy-start | bytes 786436
  5.7 1.2 %collective-permute-start = (f32[8,128]{1,0:T(8,128)S(1)}, f32[8,128]{1,0:T(8,128)S(1)}, u32[]{:S(2)}, u32[]{:S(2)}) collective-permute-start(f32[8,128]{1,0:T(8,128)S(1)} %get-tuple-element.14.mine_ref), channel_id=1, source_target_pairs={{0,16},{16,0},{1,17},{17,1},{2,18},{18,2},{3,19},{19,3},{4,20},{20... | collective-permute-start | bytes 12296 | tf_op jit(solution)/shard_map/ppermute | solution.py:202
  7.1 12.3 %collective-permute-start.11 = (bf16[528,256]{1,0:T(8,128)(2,1)S(1)}, bf16[528,256]{1,0:T(8,128)(2,1)S(1)}, u32[]{:S(2)}, u32[]{:S(2)}) collective-permute-start(bf16[528,256]{1,0:T(8,128)(2,1)S(1)} %get-tuple-element.15.im_ref.refs_6_), channel_id=1, source_target_pairs={{0,12},{1,13},{2,14},{3,15},{4,0},{5,1},{6,2},{7,3},{8,4},{9,5},{1... | collective-permute-start | bytes 811016 | tf_op jit(solution)/shard_map/ppermute | solution.py:171
  10.6 12.1 %collective-permute-start.6 = (bf16[512,256]{1,0:T(8,128)(2,1)S(1)}, bf16[512,256]{1,0:T(8,128)(2,1)S(1)}, u32[]{:S(2)}, u32[]{:S(2)}) collective-permute-start(bf16[512,256]{1,0:T(8,128)(2,1)S(1)} %collective-permute-done.1.refs_1_), channel_id=1, source_target_pairs={{0,12},{1,13},{2,14},{3,15},{4,0},{5,1},{6,2},{7,3},{8,4},{9,5},{1... | collective-permute-start | bytes 786440 | tf_op jit(solution)/shard_map/ppermute | solution.py:171
  14.8 10.3 %collective-permute-start.5 = (bf16[512,256]{1,0:T(8,128)(2,1)S(1)}, bf16[512,256]{1,0:T(8,128)(2,1)S(1)}, u32[]{:S(2)}, u32[]{:S(2)}) collective-permute-start(bf16[512,256]{1,0:T(8,128)(2,1)S(1)} %collective-permute-done.1.refs_1_), channel_id=1, source_target_pairs={{0,1},{1,0},{2,3},{3,2},{4,5},{5,4},{6,7},{7,6},{8,9},{9,8},{10,11... | collective-permute-start | bytes 786440 | tf_op jit(solution)/shard_map/ppermute | solution.py:171
  15.3 10.3 %collective-permute-start.3 = (bf16[512,256]{1,0:T(8,128)(2,1)S(1)}, bf16[512,256]{1,0:T(8,128)(2,1)S(1)}, u32[]{:S(2)}, u32[]{:S(2)}) collective-permute-start(bf16[512,256]{1,0:T(8,128)(2,1)S(1)} %get-tuple-element.12.re_ref.refs_0_), channel_id=1, source_target_pairs={{2,0},{3,1},{6,4},{7,5},{10,8},{11,9},{14,12},{15,13},{18,16},{19,... | collective-permute-start | bytes 786440 | tf_op jit(solution)/shard_map/ppermute | solution.py:171
  16.6 11.7 %collective-permute-start.2 = (bf16[512,256]{1,0:T(8,128)(2,1)S(1)}, bf16[512,256]{1,0:T(8,128)(2,1)S(1)}, u32[]{:S(2)}, u32[]{:S(2)}) collective-permute-start(bf16[512,256]{1,0:T(8,128)(2,1)S(1)} %collective-permute-done.1.refs_1_), channel_id=1, source_target_pairs={{0,2},{1,3},{2,0},{3,1},{4,6},{5,7},{6,4},{7,5},{8,10},{9,11},{10,... | collective-permute-start | bytes 786440 | tf_op jit(solution)/shard_map/ppermute | solution.py:171
  19.3 34.5 %collective-permute-start.8 = (bf16[512,256]{1,0:T(8,128)(2,1)S(1)}, bf16[512,256]{1,0:T(8,128)(2,1)S(1)}, u32[]{:S(2)}, u32[]{:S(2)}) collective-permute-start(bf16[512,256]{1,0:T(8,128)(2,1)S(1)} %get-tuple-element.12.re_ref.refs_0_), channel_id=1, source_target_pairs={{1,0},{3,2},{5,4},{7,6},{9,8},{11,10},{13,12},{15,14},{17,16},{19,... | collective-permute-start | bytes 786440 | tf_op jit(solution)/shard_map/ppermute | solution.py:171
  22.8 7.2 %collective-permute-start.16 = (bf16[528,256]{1,0:T(8,128)(2,1)S(1)}, bf16[528,256]{1,0:T(8,128)(2,1)S(1)}, u32[]{:S(2)}, u32[]{:S(2)}) collective-permute-start(bf16[528,256]{1,0:T(8,128)(2,1)S(1)} %collective-permute-done.11.refs_7_), channel_id=1, source_target_pairs={{0,12},{1,13},{2,14},{3,15},{4,0},{5,1},{6,2},{7,3},{8,4},{9,5},{1... | collective-permute-start | bytes 811016 | tf_op jit(solution)/shard_map/ppermute | solution.py:171
  25.1 7.3 %collective-permute-start.15 = (bf16[528,256]{1,0:T(8,128)(2,1)S(1)}, bf16[528,256]{1,0:T(8,128)(2,1)S(1)}, u32[]{:S(2)}, u32[]{:S(2)}) collective-permute-start(bf16[528,256]{1,0:T(8,128)(2,1)S(1)} %collective-permute-done.11.refs_7_), channel_id=1, source_target_pairs={{0,1},{1,0},{2,3},{3,2},{4,5},{5,4},{6,7},{7,6},{8,9},{9,8},{10,11... | collective-permute-start | bytes 811016 | tf_op jit(solution)/shard_map/ppermute | solution.py:171
  25.7 11.2 %collective-permute-start.13 = (bf16[528,256]{1,0:T(8,128)(2,1)S(1)}, bf16[528,256]{1,0:T(8,128)(2,1)S(1)}, u32[]{:S(2)}, u32[]{:S(2)}) collective-permute-start(bf16[528,256]{1,0:T(8,128)(2,1)S(1)} %get-tuple-element.15.im_ref.refs_6_), channel_id=1, source_target_pairs={{2,0},{3,1},{6,4},{7,5},{10,8},{11,9},{14,12},{15,13},{18,16},{19,... | collective-permute-start | bytes 811016 | tf_op jit(solution)/shard_map/ppermute | solution.py:171
  28.3 14.4 %collective-permute-start.12 = (bf16[528,256]{1,0:T(8,128)(2,1)S(1)}, bf16[528,256]{1,0:T(8,128)(2,1)S(1)}, u32[]{:S(2)}, u32[]{:S(2)}) collective-permute-start(bf16[528,256]{1,0:T(8,128)(2,1)S(1)} %collective-permute-done.11.refs_7_), channel_id=1, source_target_pairs={{0,2},{1,3},{2,0},{3,1},{4,6},{5,7},{6,4},{7,5},{8,10},{9,11},{10,... | collective-permute-start | bytes 811016 | tf_op jit(solution)/shard_map/ppermute | solution.py:171
  30.0 18.4 %collective-permute-start.7 = (bf16[512,256]{1,0:T(8,128)(2,1)S(1)}, bf16[512,256]{1,0:T(8,128)(2,1)S(1)}, u32[]{:S(2)}, u32[]{:S(2)}) collective-permute-start(bf16[512,256]{1,0:T(8,128)(2,1)S(1)} %broadcast_select_fusion.3), channel_id=1, source_target_pairs={{0,2},{1,3},{2,0},{3,1},{4,6},{5,7},{6,4},{7,5},{8,10},{9,11},{10,... | collective-permute-start | bytes 786440 | tf_op jit(solution)/shard_map/ppermute | solution.py:171
  32.4 17.5 %collective-permute-start.4 = (bf16[512,256]{1,0:T(8,128)(2,1)S(1)}, bf16[512,256]{1,0:T(8,128)(2,1)S(1)}, u32[]{:S(2)}, u32[]{:S(2)}) collective-permute-start(bf16[512,256]{1,0:T(8,128)(2,1)S(1)} %broadcast_select_fusion.4), channel_id=1, source_target_pairs={{0,1},{1,0},{2,3},{3,2},{4,5},{5,4},{6,7},{7,6},{8,9},{9,8},{10,11... | collective-permute-start | bytes 786440 | tf_op jit(solution)/shard_map/ppermute | solution.py:171
  36.9 22.9 %collective-permute-start.17 = (bf16[528,256]{1,0:T(8,128)(2,1)S(1)}, bf16[528,256]{1,0:T(8,128)(2,1)S(1)}, u32[]{:S(2)}, u32[]{:S(2)}) collective-permute-start(bf16[528,256]{1,0:T(8,128)(2,1)S(1)} %broadcast_select_fusion), channel_id=1, source_target_pairs={{0,2},{1,3},{2,0},{3,1},{4,6},{5,7},{6,4},{7,5},{8,10},{9,11},{10,... | collective-permute-start | bytes 811016 | tf_op jit(solution)/shard_map/ppermute | solution.py:171
  42.7 9.7 %collective-permute-start.18 = (bf16[528,256]{1,0:T(8,128)(2,1)S(1)}, bf16[528,256]{1,0:T(8,128)(2,1)S(1)}, u32[]{:S(2)}, u32[]{:S(2)}) collective-permute-start(bf16[528,256]{1,0:T(8,128)(2,1)S(1)} %collective-permute-done.15.refs_9_), channel_id=1, source_target_pairs={{0,12},{1,13},{3,15},{4,0},{5,1},{7,3},{8,4},{9,5},{11,7},{12,8},{... | collective-permute-start | bytes 811016 | tf_op jit(solution)/shard_map/ppermute | solution.py:171
  48.3 11.5 %collective-permute-start.14 = (bf16[528,256]{1,0:T(8,128)(2,1)S(1)}, bf16[528,256]{1,0:T(8,128)(2,1)S(1)}, u32[]{:S(2)}, u32[]{:S(2)}) collective-permute-start(bf16[528,256]{1,0:T(8,128)(2,1)S(1)} %broadcast_select_fusion.1), channel_id=1, source_target_pairs={{0,1},{1,0},{2,3},{3,2},{4,5},{5,4},{6,7},{7,6},{8,9},{9,8},{10,11... | collective-permute-start | bytes 811016 | tf_op jit(solution)/shard_map/ppermute | solution.py:171
  49.9 12.3 %collective-permute-start.10 = (bf16[528,256]{1,0:T(8,128)(2,1)S(1)}, bf16[528,256]{1,0:T(8,128)(2,1)S(1)}, u32[]{:S(2)}, u32[]{:S(2)}) collective-permute-start(bf16[528,256]{1,0:T(8,128)(2,1)S(1)} %pad_select_fusion), channel_id=1, source_target_pairs={{1,0},{2,3},{3,2},{5,4},{6,7},{7,6},{9,8},{10,11},{11,10},{13,12},... | collective-permute-start | bytes 811016 | tf_op jit(solution)/shard_map/ppermute | solution.py:171
  52.4 9.8 %collective-permute-start.19 = (bf16[528,256]{1,0:T(8,128)(2,1)S(1)}, bf16[528,256]{1,0:T(8,128)(2,1)S(1)}, u32[]{:S(2)}, u32[]{:S(2)}) collective-permute-start(bf16[528,256]{1,0:T(8,128)(2,1)S(1)} %collective-permute-done.18.refs_9_), channel_id=1, source_target_pairs={{0,2},{1,3},{4,6},{5,7},{8,10},{9,11},{12,14},{13,15},{16,18},{17,... | collective-permute-start | bytes 811016 | tf_op jit(solution)/shard_map/ppermute | solution.py:171
  53.9 8.3 %collective-permute-start.9 = (bf16[512,256]{1,0:T(8,128)(2,1)S(1)}, bf16[512,256]{1,0:T(8,128)(2,1)S(1)}, u32[]{:S(2)}, u32[]{:S(2)}) collective-permute-start(bf16[512,256]{1,0:T(8,128)(2,1)S(1)} %broadcast_select_fusion.2), channel_id=1, source_target_pairs={{1,13},{2,14},{3,15},{5,1},{6,2},{7,3},{9,5},{10,6},{11,7},{13,9},... | collective-permute-start | bytes 786440 | tf_op jit(solution)/shard_map/ppermute | solution.py:171

commit v2 on v1

--- a/solution.py
+++ b/solution.py
@@ -11,7 +11,7 @@
 
 BLOCKS = ("sr", "sc")
 GAIN_PARTS = 3
-GAIN_ROWS = 16
+GAIN_ROWS = 8
 VMEM_BYTES = 16 << 20
 CHUNK = 8
 
@@ -72,16 +72,15 @@
     contract = (((1,), (1,)), ((), ()))
     column = lax.axis_index("sc")
 
+    place = lax.broadcasted_iota(jnp.int32, offsets_ref.shape, 1)
     wanted, slots = [], []
     for entry in entries:
         offset, use = entry(column)
         use = jnp.logical_and(use, jnp.logical_and(offset >= 0, offset < slot_count))
 
-        def find(m, found, offset=offset):
-            return jnp.where(offsets_ref[0, m] == offset, m, found)
-
+        hit = offsets_ref[...] == offset
         wanted.append(use)
-        slots.append(lax.fori_loop(0, slot_count, find, jnp.int32(0), unroll=True))
+        slots.append(jnp.sum(jnp.where(hit, place, 0)))
 
     def copy_out(i, f):
         return pltpu.make_async_copy(
@@ -122,7 +121,7 @@
     count = len(group)
     args = [offsets, *own, weight]
     args += [pair[0] for pair, _ in group] + [pair[1] for pair, _ in group]
-    specs = [pl.BlockSpec(memory_space=pltpu.SMEM)] + [vmem()] * (len(args) - 1)
+    specs = [vmem()] * len(args)
     aliases = {}
     if out is not None:
         aliases = {len(args): 0}
@@ -256,10 +255,9 @@
         d = both(v, flip(1))
         soon_group += [(p, entry(j, bit)) for bit, p in enumerate((planes[j], u, v, d))]
     groups = [soon_group[i : i + CHUNK] for i in range(0, len(soon_group), CHUNK)]
+    groups.append([(x3, x3_entry), (y3, y3_entry)])
     groups.append(
         [
-            (x3, x3_entry),
-            (y3, y3_entry),
             ((u1a, xl), entry(0, 1)),
             ((z3a, z3b), entry(half, 1, lambda column: (column & 1) == 1)),
             ((z3a, yfb), entry(half, 3, lambda column: column == 2)),

time: 65 us -> 61.6 us (0.948)
  the two profiles are of different devices: /device:TPU:2 before, /device:TPU:10 now
where the time goes in v2:
time: 61.6 us; the launch traced here: 61.3 us
  starting transfers between devices  29.3 us (48%)
  waiting for transfers between devices  23.6 us (38%)
  Pallas kernels  6.09 us (10%)
  local copies, waits for them, and re-layouts  1.9 us (3%)
    ppermute x19, starting transfers between devices, send(): return lax.ppermute(value, BLOCKS, links)  29.2 us
    ppermute x19, waiting for transfers between devices, send(): return lax.ppermute(value, BLOCKS, links)  22.4 us
    pallas_call x3, Pallas kernels, products(): pl.pallas_call(functools.partial(product_kernel, [entry for _, entry in g...  5.76 us
    unnamed x6, local copies, waits for them, and re-layouts  1.9 us
  transfers between devices with their start and end apart: 20, of which 9 were waited for; matrix products, arithmetic and copies ran while one was open for 0% of the time, Pallas kernels for 8%

profile of v2, /device:TPU:10, one launch (start us, length us, event | category | flops | bytes accessed | tf_op | source)
XLA Modules:
  0.0 61.3 jit_solution(7577781138767035516)
XLA Ops:
  0.0 0.4 collective-permute-start.2
  0.5 0.9 %copy-done = bf16[4,128,256]{2,1,0:T(8,128)(2,1)S(1)} copy-done((bf16[4,128,256]{2,1,0:T(8,128)(2,1)S(1)}, bf16[4,128,256]{2,1,0:T(8,128)(2,1)}, u32[]{:S(2)}) %copy-start) | copy-done | bytes 262168
  1.4 0.9 %copy-done.1 = bf16[4,128,256]{2,1,0:T(8,128)(2,1)S(1)} copy-done((bf16[4,128,256]{2,1,0:T(8,128)(2,1)S(1)}, bf16[4,128,256]{2,1,0:T(8,128)(2,1)}, u32[]{:S(2)}) %copy-start.1) | copy-done | bytes 262168
  2.4 0.2 power.1
  2.6 0.1 collective-permute-start
  2.7 1.2 %collective-permute-done.other_ref = f32[8,128]{1,0:T(8,128)S(1)} collective-permute-done((f32[8,128]{1,0:T(8,128)S(1)}, f32[8,128]{1,0:T(8,128)S(1)}, u32[]{:S(2)}, u32[]{:S(2)}) %collective-permute-start) | collective-permute-done | bytes 4128 | tf_op jit(solution)/shard_map/ppermute | solution.py:201
  3.8 0.1 cat.1
  3.9 3.7 %collective-permute-start.11 = (bf16[520,256]{1,0:T(8,128)(2,1)S(1)}, bf16[520,256]{1,0:T(8,128)(2,1)S(1)}, u32[]{:S(2)}, u32[]{:S(2)}) collective-permute-start(bf16[520,256]{1,0:T(8,128)(2,1)S(1)} %get-tuple-element.15.im_ref.refs_6_), channel_id=1, source_target_pairs={{0,12},{1,13},{2,14},{3,15},{4,0},{5,1},{6,2},{7,3},{8,4},{9,5},{1... | collective-permute-start | bytes 798728 | tf_op jit(solution)/shard_map/ppermute | solution.py:170
  7.6 1.3 %collective-permute-start.4 = (bf16[512,256]{1,0:T(8,128)(2,1)S(1)}, bf16[512,256]{1,0:T(8,128)(2,1)S(1)}, u32[]{:S(2)}, u32[]{:S(2)}) collective-permute-start(bf16[512,256]{1,0:T(8,128)(2,1)S(1)} %get-tuple-element.12.re_ref.refs_0_), channel_id=1, source_target_pairs={{2,0},{3,1},{6,4},{7,5},{10,8},{11,9},{14,12},{15,13},{18,16},{19,... | collective-permute-start | bytes 786440 | tf_op jit(solution)/shard_map/ppermute | solution.py:170
  8.9 0.5 collective-permute-done.2.refs_1_
  9.4 2.2 %collective-permute-start.3 = (bf16[512,256]{1,0:T(8,128)(2,1)S(1)}, bf16[512,256]{1,0:T(8,128)(2,1)S(1)}, u32[]{:S(2)}, u32[]{:S(2)}) collective-permute-start(bf16[512,256]{1,0:T(8,128)(2,1)S(1)} %collective-permute-done.2.refs_1_), channel_id=1, source_target_pairs={{0,2},{1,3},{2,0},{3,1},{4,6},{5,7},{6,4},{7,5},{8,10},{9,11},{10,... | collective-permute-start | bytes 786440 | tf_op jit(solution)/shard_map/ppermute | solution.py:170
  11.6 0.5 collective-permute-start.6
  12.1 1.0 %collective-permute-start.8 = (bf16[512,256]{1,0:T(8,128)(2,1)S(1)}, bf16[512,256]{1,0:T(8,128)(2,1)S(1)}, u32[]{:S(2)}, u32[]{:S(2)}) collective-permute-start(bf16[512,256]{1,0:T(8,128)(2,1)S(1)} %collective-permute-done.2.refs_1_), channel_id=1, source_target_pairs={{0,12},{1,13},{2,14},{3,15},{4,0},{5,1},{6,2},{7,3},{8,4},{9,5},{1... | collective-permute-start | bytes 786440 | tf_op jit(solution)/shard_map/ppermute | solution.py:170
  13.1 5.5 %collective-permute-done.4.refs_2_ = bf16[512,256]{1,0:T(8,128)(2,1)S(1)} collective-permute-done((bf16[512,256]{1,0:T(8,128)(2,1)S(1)}, bf16[512,256]{1,0:T(8,128)(2,1)S(1)}, u32[]{:S(2)}, u32[]{:S(2)}) %collective-permute-start.4) | collective-permute-done | bytes 262176 | tf_op jit(solution)/shard_map/ppermute | solution.py:170
  18.6 2.4 %collective-permute-start.1 = (bf16[512,256]{1,0:T(8,128)(2,1)S(1)}, bf16[512,256]{1,0:T(8,128)(2,1)S(1)}, u32[]{:S(2)}, u32[]{:S(2)}) collective-permute-start(bf16[512,256]{1,0:T(8,128)(2,1)S(1)} %get-tuple-element.12.re_ref.refs_0_), channel_id=1, source_target_pairs={{1,0},{3,2},{5,4},{7,6},{9,8},{11,10},{13,12},{15,14},{17,16},{19,... | collective-permute-start | bytes 786440 | tf_op jit(solution)/shard_map/ppermute | solution.py:170
  21.1 0.0 collective-permute-done.11.refs_7_
  21.1 0.1 collective-permute-start.12
  21.2 2.0 %collective-permute-done.3.refs_4_ = bf16[512,256]{1,0:T(8,128)(2,1)S(1)} collective-permute-done((bf16[512,256]{1,0:T(8,128)(2,1)S(1)}, bf16[512,256]{1,0:T(8,128)(2,1)S(1)}, u32[]{:S(2)}, u32[]{:S(2)}) %collective-permute-start.3) | collective-permute-done | bytes 262176 | tf_op jit(solution)/shard_map/ppermute | solution.py:170
  23.2 0.4 collective-permute-start.18
  23.7 0.0 collective-permute-done.6.refs_3_
  23.7 1.3 %collective-permute-start.16 = (bf16[520,256]{1,0:T(8,128)(2,1)S(1)}, bf16[520,256]{1,0:T(8,128)(2,1)S(1)}, u32[]{:S(2)}, u32[]{:S(2)}) collective-permute-start(bf16[520,256]{1,0:T(8,128)(2,1)S(1)} %get-tuple-element.15.im_ref.refs_6_), channel_id=1, source_target_pairs={{2,0},{3,1},{6,4},{7,5},{10,8},{11,9},{14,12},{15,13},{18,16},{19,... | collective-permute-start | bytes 798728 | tf_op jit(solution)/shard_map/ppermute | solution.py:170
  25.0 0.0 collective-permute-done.8.refs_5_
  25.0 2.7 %collective-permute-start.15 = (bf16[520,256]{1,0:T(8,128)(2,1)S(1)}, bf16[520,256]{1,0:T(8,128)(2,1)S(1)}, u32[]{:S(2)}, u32[]{:S(2)}) collective-permute-start(bf16[520,256]{1,0:T(8,128)(2,1)S(1)} %collective-permute-done.11.refs_7_), channel_id=1, source_target_pairs={{0,2},{1,3},{2,0},{3,1},{4,6},{5,7},{6,4},{7,5},{8,10},{9,11},{10,... | collective-permute-start | bytes 798728 | tf_op jit(solution)/shard_map/ppermute | solution.py:170
  27.7 3.0 %collective-permute-done.12.refs_9_ = bf16[520,256]{1,0:T(8,128)(2,1)S(1)} collective-permute-done((bf16[520,256]{1,0:T(8,128)(2,1)S(1)}, bf16[520,256]{1,0:T(8,128)(2,1)S(1)}, u32[]{:S(2)}, u32[]{:S(2)}) %collective-permute-start.12) | collective-permute-done | bytes 266272 | tf_op jit(solution)/shard_map/ppermute | solution.py:170
  30.8 2.5 %collective-permute-start.5 = (bf16[512,256]{1,0:T(8,128)(2,1)S(1)}, bf16[512,256]{1,0:T(8,128)(2,1)S(1)}, u32[]{:S(2)}, u32[]{:S(2)}) collective-permute-start(bf16[512,256]{1,0:T(8,128)(2,1)S(1)} %broadcast_select_fusion.3), channel_id=1, source_target_pairs={{0,1},{1,0},{2,3},{3,2},{4,5},{5,4},{6,7},{7,6},{8,9},{9,8},{10,11... | collective-permute-start | bytes 786440 | tf_op jit(solution)/shard_map/ppermute | solution.py:170
  33.2 0.0 collective-permute-done.18.refs_11_
  33.2 0.0 collective-permute-start.9
  33.3 1.6 %collective-permute-done.16.refs_8_ = bf16[520,256]{1,0:T(8,128)(2,1)S(1)} collective-permute-done((bf16[520,256]{1,0:T(8,128)(2,1)S(1)}, bf16[520,256]{1,0:T(8,128)(2,1)S(1)}, u32[]{:S(2)}, u32[]{:S(2)}) %collective-permute-start.16) | collective-permute-done | bytes 266272 | tf_op jit(solution)/shard_map/ppermute | solution.py:170
  34.8 0.5 collective-permute-start.19
  35.4 5.2 %collective-permute-done.15.refs_10_ = bf16[520,256]{1,0:T(8,128)(2,1)S(1)} collective-permute-done((bf16[520,256]{1,0:T(8,128)(2,1)S(1)}, bf16[520,256]{1,0:T(8,128)(2,1)S(1)}, u32[]{:S(2)}, u32[]{:S(2)}) %collective-permute-start.15) | collective-permute-done | bytes 266272 | tf_op jit(solution)/shard_map/ppermute | solution.py:170
  40.5 2.3 %collective-permute-start.13 = (bf16[520,256]{1,0:T(8,128)(2,1)S(1)}, bf16[520,256]{1,0:T(8,128)(2,1)S(1)}, u32[]{:S(2)}, u32[]{:S(2)}) collective-permute-start(bf16[520,256]{1,0:T(8,128)(2,1)S(1)} %collective-permute-done.12.refs_9_), channel_id=1, source_target_pairs={{0,12},{1,13},{3,15},{4,0},{5,1},{7,3},{8,4},{9,5},{11,7},{12,8},{... | collective-permute-start | bytes 798728 | tf_op jit(solution)/shard_map/ppermute | solution.py:170
  42.9 3.2 %collective-permute-done.9.refs_1_ = bf16[512,256]{1,0:T(8,128)(2,1)S(1)} collective-permute-done((bf16[512,256]{1,0:T(8,128)(2,1)S(1)}, bf16[512,256]{1,0:T(8,128)(2,1)S(1)}, u32[]{:S(2)}, u32[]{:S(2)}) %collective-permute-start.9) | collective-permute-done | bytes 262176 | tf_op jit(solution)/shard_map/ppermute | solution.py:170
  46.2 0.5 collective-permute-start.17
  46.7 0.1 pad_select_fusion
  46.8 0.0 collective-permute-done.5.refs_0_
  46.8 3.4 %collective-permute-start.10 = (bf16[520,256]{1,0:T(8,128)(2,1)S(1)}, bf16[520,256]{1,0:T(8,128)(2,1)S(1)}, u32[]{:S(2)}, u32[]{:S(2)}) collective-permute-start(bf16[520,256]{1,0:T(8,128)(2,1)S(1)} %pad_select_fusion), channel_id=1, source_target_pairs={{1,0},{2,3},{3,2},{5,4},{6,7},{7,6},{9,8},{10,11},{11,10},{13,12},... | collective-permute-start | bytes 798728 | tf_op jit(solution)/shard_map/ppermute | solution.py:170
  50.2 0.0 collective-permute-done.13.refs_5_
  50.2 1.5 %collective-permute-start.14 = (bf16[520,256]{1,0:T(8,128)(2,1)S(1)}, bf16[520,256]{1,0:T(8,128)(2,1)S(1)}, u32[]{:S(2)}, u32[]{:S(2)}) collective-permute-start(bf16[520,256]{1,0:T(8,128)(2,1)S(1)} %collective-permute-done.13.refs_5_), channel_id=1, source_target_pairs={{0,2},{1,3},{4,6},{5,7},{8,10},{9,11},{12,14},{13,15},{16,18},{17,... | collective-permute-start | bytes 798728 | tf_op jit(solution)/shard_map/ppermute | solution.py:170
  51.7 0.0 collective-permute-done.19.refs_3_
  51.7 2.4 %collective-permute-start.7 = (bf16[512,256]{1,0:T(8,128)(2,1)S(1)}, bf16[512,256]{1,0:T(8,128)(2,1)S(1)}, u32[]{:S(2)}, u32[]{:S(2)}) collective-permute-start(bf16[512,256]{1,0:T(8,128)(2,1)S(1)} %broadcast_select_fusion.4), channel_id=1, source_target_pairs={{1,13},{2,14},{3,15},{5,1},{6,2},{7,3},{9,5},{10,6},{11,7},{13,9},... | collective-permute-start | bytes 786440 | tf_op jit(solution)/shard_map/ppermute | solution.py:170
  54.1 2.8 %shard_map.37.refs_4_ = f32[4,1,9,128,256]{4,3,2,1,0:T(8,128)} custom-call(s32[1,9]{1,0:T(1,128)S(1)} %copy-done.2, bf16[512,256]{1,0:T(8,128)(2,1)S(1)} %get-tuple-element.12.re_ref.refs_0_, bf16[520,256]{1,0:T(8,128)(2,1)S(1)} %get-tuple-element.15.im_ref.refs_6_, f32[128,128]{1,0:T(8,128)S(1)} %get-tuple-element.16.weight_ref, ...), custom_call_target="tpu_custom_call" | custom-call | flops 805306368 | bytes 3145728 | tf_op jit(solution)/shard_map/pallas_call | solution.py:130
  56.9 0.0 collective-permute-done.17.refs_2_
  56.9 1.6 %shard_map.38.refs_8_ = f32[4,1,9,128,256]{4,3,2,1,0:T(8,128)} custom-call(s32[1,9]{1,0:T(1,128)S(1)} %copy-done.2, bf16[512,256]{1,0:T(8,128)(2,1)S(1)} %get-tuple-element.12.re_ref.refs_0_, bf16[520,256]{1,0:T(8,128)(2,1)S(1)} %get-tuple-element.15.im_ref.refs_6_, f32[128,128]{1,0:T(8,128)S(1)} %get-tuple-element.16.weight_ref, ...), custom_call_target="tpu_custom_call", output_to_operand_aliasing={{}: (8, {})} | custom-call | flops 268435456 | bytes 1048576 | tf_op jit(solution)/shard_map/pallas_call | solution.py:130
  58.5 0.0 collective-permute-done.1.refs_0_
  58.6 1.4 %collective-permute-done.7.refs_1_.refs_2_ = bf16[512,256]{1,0:T(8,128)(2,1)S(1)} collective-permute-done((bf16[512,256]{1,0:T(8,128)(2,1)S(1)}, bf16[512,256]{1,0:T(8,128)(2,1)S(1)}, u32[]{:S(2)}, u32[]{:S(2)}) %collective-permute-start.7) | collective-permute-done | bytes 262176 | tf_op jit(solution)/shard_map/ppermute | solution.py:170
  60.0 0.0 collective-permute-done.10.refs_3_.refs_4_
  60.0 0.0 collective-permute-done.14.refs_6_.refs_7_
  60.0 1.3 %shard_map.39 = f32[4,1,9,128,256]{4,3,2,1,0:T(8,128)} custom-call(s32[1,9]{1,0:T(1,128)S(1)} %copy-done.2, bf16[512,256]{1,0:T(8,128)(2,1)S(1)} %get-tuple-element.12.re_ref.refs_0_, bf16[520,256]{1,0:T(8,128)(2,1)S(1)} %get-tuple-element.15.im_ref.refs_6_, f32[128,128]{1,0:T(8,128)S(1)} %get-tuple-element.16.weight_ref, ...), custom_call_target="tpu_custom_call", output_to_operand_aliasing={{}: (12, {})} | custom-call | flops 536870912 | bytes 2097152 | tf_op jit(solution)/shard_map/pallas_call | solution.py:130
  (9 shorter events, 0.2 us)
Async XLA Ops:
  0.0 54.1 %copy-start.2 = (s32[1,9]{1,0:T(1,128)S(1)}, s32[1,9]{1,0:T(1,128)}, u32[]{:S(2)}) copy-start(s32[1,9]{1,0:T(1,128)} %offsets_ref.5) | copy-start | bytes 112
  0.0 9.4 %collective-permute-start.2 = (bf16[512,256]{1,0:T(8,128)(2,1)}, bf16[512,256]{1,0:T(8,128)(2,1)S(1)}, u32[]{:S(2)}, u32[]{:S(2)}) collective-permute-start(bf16[512,256]{1,0:T(8,128)(2,1)} %bitcast.3), channel_id=1, source_target_pairs={{0,12},{1,13},{2,14},{3,15},{4,0},{5,1},{6,2},{7,3},{8,4},{9,5},{1... | collective-permute-start | bytes 786440 | tf_op jit(solution)/shard_map/ppermute | solution.py:170
  0.5 0.9 %copy-start = (bf16[4,128,256]{2,1,0:T(8,128)(2,1)S(1)}, bf16[4,128,256]{2,1,0:T(8,128)(2,1)}, u32[]{:S(2)}) copy-start(bf16[4,128,256]{2,1,0:T(8,128)(2,1)} %param.4) | copy-start | bytes 786436
  1.4 0.9 %copy-start.1 = (bf16[4,128,256]{2,1,0:T(8,128)(2,1)S(1)}, bf16[4,128,256]{2,1,0:T(8,128)(2,1)}, u32[]{:S(2)}) copy-start(bf16[4,128,256]{2,1,0:T(8,128)(2,1)} %param.3) | copy-start | bytes 786436
  2.6 1.2 %collective-permute-start = (f32[8,128]{1,0:T(8,128)S(1)}, f32[8,128]{1,0:T(8,128)S(1)}, u32[]{:S(2)}, u32[]{:S(2)}) collective-permute-start(f32[8,128]{1,0:T(8,128)S(1)} %get-tuple-element.14.mine_ref), channel_id=1, source_target_pairs={{0,16},{16,0},{1,17},{17,1},{2,18},{18,2},{3,19},{19,3},{4,20},{20... | collective-permute-start | bytes 12296 | tf_op jit(solution)/shard_map/ppermute | solution.py:201
  3.9 17.2 %collective-permute-start.11 = (bf16[520,256]{1,0:T(8,128)(2,1)S(1)}, bf16[520,256]{1,0:T(8,128)(2,1)S(1)}, u32[]{:S(2)}, u32[]{:S(2)}) collective-permute-start(bf16[520,256]{1,0:T(8,128)(2,1)S(1)} %get-tuple-element.15.im_ref.refs_6_), channel_id=1, source_target_pairs={{0,12},{1,13},{2,14},{3,15},{4,0},{5,1},{6,2},{7,3},{8,4},{9,5},{1... | collective-permute-start | bytes 798728 | tf_op jit(solution)/shard_map/ppermute | solution.py:170
  7.6 11.1 %collective-permute-start.4 = (bf16[512,256]{1,0:T(8,128)(2,1)S(1)}, bf16[512,256]{1,0:T(8,128)(2,1)S(1)}, u32[]{:S(2)}, u32[]{:S(2)}) collective-permute-start(bf16[512,256]{1,0:T(8,128)(2,1)S(1)} %get-tuple-element.12.re_ref.refs_0_), channel_id=1, source_target_pairs={{2,0},{3,1},{6,4},{7,5},{10,8},{11,9},{14,12},{15,13},{18,16},{19,... | collective-permute-start | bytes 786440 | tf_op jit(solution)/shard_map/ppermute | solution.py:170
  9.4 13.8 %collective-permute-start.3 = (bf16[512,256]{1,0:T(8,128)(2,1)S(1)}, bf16[512,256]{1,0:T(8,128)(2,1)S(1)}, u32[]{:S(2)}, u32[]{:S(2)}) collective-permute-start(bf16[512,256]{1,0:T(8,128)(2,1)S(1)} %collective-permute-done.2.refs_1_), channel_id=1, source_target_pairs={{0,2},{1,3},{2,0},{3,1},{4,6},{5,7},{6,4},{7,5},{8,10},{9,11},{10,... | collective-permute-start | bytes 786440 | tf_op jit(solution)/shard_map/ppermute | solution.py:170
  11.6 12.1 %collective-permute-start.6 = (bf16[512,256]{1,0:T(8,128)(2,1)S(1)}, bf16[512,256]{1,0:T(8,128)(2,1)S(1)}, u32[]{:S(2)}, u32[]{:S(2)}) collective-permute-start(bf16[512,256]{1,0:T(8,128)(2,1)S(1)} %collective-permute-done.2.refs_1_), channel_id=1, source_target_pairs={{0,1},{1,0},{2,3},{3,2},{4,5},{5,4},{6,7},{7,6},{8,9},{9,8},{10,11... | collective-permute-start | bytes 786440 | tf_op jit(solution)/shard_map/ppermute | solution.py:170
  12.1 12.8 %collective-permute-start.8 = (bf16[512,256]{1,0:T(8,128)(2,1)S(1)}, bf16[512,256]{1,0:T(8,128)(2,1)S(1)}, u32[]{:S(2)}, u32[]{:S(2)}) collective-permute-start(bf16[512,256]{1,0:T(8,128)(2,1)S(1)} %collective-permute-done.2.refs_1_), channel_id=1, source_target_pairs={{0,12},{1,13},{2,14},{3,15},{4,0},{5,1},{6,2},{7,3},{8,4},{9,5},{1... | collective-permute-start | bytes 786440 | tf_op jit(solution)/shard_map/ppermute | solution.py:170
  18.6 39.9 %collective-permute-start.1 = (bf16[512,256]{1,0:T(8,128)(2,1)S(1)}, bf16[512,256]{1,0:T(8,128)(2,1)S(1)}, u32[]{:S(2)}, u32[]{:S(2)}) collective-permute-start(bf16[512,256]{1,0:T(8,128)(2,1)S(1)} %get-tuple-element.12.re_ref.refs_0_), channel_id=1, source_target_pairs={{1,0},{3,2},{5,4},{7,6},{9,8},{11,10},{13,12},{15,14},{17,16},{19,... | collective-permute-start | bytes 786440 | tf_op jit(solution)/shard_map/ppermute | solution.py:170
  21.1 9.7 %collective-permute-start.12 = (bf16[520,256]{1,0:T(8,128)(2,1)S(1)}, bf16[520,256]{1,0:T(8,128)(2,1)S(1)}, u32[]{:S(2)}, u32[]{:S(2)}) collective-permute-start(bf16[520,256]{1,0:T(8,128)(2,1)S(1)} %collective-permute-done.11.refs_7_), channel_id=1, source_target_pairs={{0,1},{1,0},{2,3},{3,2},{4,5},{5,4},{6,7},{7,6},{8,9},{9,8},{10,11... | collective-permute-start | bytes 798728 | tf_op jit(solution)/shard_map/ppermute | solution.py:170
  23.2 10.1 %collective-permute-start.18 = (bf16[520,256]{1,0:T(8,128)(2,1)S(1)}, bf16[520,256]{1,0:T(8,128)(2,1)S(1)}, u32[]{:S(2)}, u32[]{:S(2)}) collective-permute-start(bf16[520,256]{1,0:T(8,128)(2,1)S(1)} %collective-permute-done.11.refs_7_), channel_id=1, source_target_pairs={{0,12},{1,13},{2,14},{3,15},{4,0},{5,1},{6,2},{7,3},{8,4},{9,5},{1... | collective-permute-start | bytes 798728 | tf_op jit(solution)/shard_map/ppermute | solution.py:170
  23.7 11.2 %collective-permute-start.16 = (bf16[520,256]{1,0:T(8,128)(2,1)S(1)}, bf16[520,256]{1,0:T(8,128)(2,1)S(1)}, u32[]{:S(2)}, u32[]{:S(2)}) collective-permute-start(bf16[520,256]{1,0:T(8,128)(2,1)S(1)} %get-tuple-element.15.im_ref.refs_6_), channel_id=1, source_target_pairs={{2,0},{3,1},{6,4},{7,5},{10,8},{11,9},{14,12},{15,13},{18,16},{19,... | collective-permute-start | bytes 798728 | tf_op jit(solution)/shard_map/ppermute | solution.py:170
  25.0 15.6 %collective-permute-start.15 = (bf16[520,256]{1,0:T(8,128)(2,1)S(1)}, bf16[520,256]{1,0:T(8,128)(2,1)S(1)}, u32[]{:S(2)}, u32[]{:S(2)}) collective-permute-start(bf16[520,256]{1,0:T(8,128)(2,1)S(1)} %collective-permute-done.11.refs_7_), channel_id=1, source_target_pairs={{0,2},{1,3},{2,0},{3,1},{4,6},{5,7},{6,4},{7,5},{8,10},{9,11},{10,... | collective-permute-start | bytes 798728 | tf_op jit(solution)/shard_map/ppermute | solution.py:170
  30.8 16.0 %collective-permute-start.5 = (bf16[512,256]{1,0:T(8,128)(2,1)S(1)}, bf16[512,256]{1,0:T(8,128)(2,1)S(1)}, u32[]{:S(2)}, u32[]{:S(2)}) collective-permute-start(bf16[512,256]{1,0:T(8,128)(2,1)S(1)} %broadcast_select_fusion.3), channel_id=1, source_target_pairs={{0,1},{1,0},{2,3},{3,2},{4,5},{5,4},{6,7},{7,6},{8,9},{9,8},{10,11... | collective-permute-start | bytes 786440 | tf_op jit(solution)/shard_map/ppermute | solution.py:170
  33.2 12.9 %collective-permute-start.9 = (bf16[512,256]{1,0:T(8,128)(2,1)S(1)}, bf16[512,256]{1,0:T(8,128)(2,1)S(1)}, u32[]{:S(2)}, u32[]{:S(2)}) collective-permute-start(bf16[512,256]{1,0:T(8,128)(2,1)S(1)} %broadcast_select_fusion.2), channel_id=1, source_target_pairs={{0,2},{1,3},{2,0},{3,1},{4,6},{5,7},{6,4},{7,5},{8,10},{9,11},{10,... | collective-permute-start | bytes 786440 | tf_op jit(solution)/shard_map/ppermute | solution.py:170
  34.8 16.9 %collective-permute-start.19 = (bf16[520,256]{1,0:T(8,128)(2,1)S(1)}, bf16[520,256]{1,0:T(8,128)(2,1)S(1)}, u32[]{:S(2)}, u32[]{:S(2)}) collective-permute-start(bf16[520,256]{1,0:T(8,128)(2,1)S(1)} %broadcast_select_fusion), channel_id=1, source_target_pairs={{0,2},{1,3},{2,0},{3,1},{4,6},{5,7},{6,4},{7,5},{8,10},{9,11},{10,... | collective-permute-start | bytes 798728 | tf_op jit(solution)/shard_map/ppermute | solution.py:170
  40.5 9.7 %collective-permute-start.13 = (bf16[520,256]{1,0:T(8,128)(2,1)S(1)}, bf16[520,256]{1,0:T(8,128)(2,1)S(1)}, u32[]{:S(2)}, u32[]{:S(2)}) collective-permute-start(bf16[520,256]{1,0:T(8,128)(2,1)S(1)} %collective-permute-done.12.refs_9_), channel_id=1, source_target_pairs={{0,12},{1,13},{3,15},{4,0},{5,1},{7,3},{8,4},{9,5},{11,7},{12,8},{... | collective-permute-start | bytes 798728 | tf_op jit(solution)/shard_map/ppermute | solution.py:170
  46.2 10.8 %collective-permute-start.17 = (bf16[520,256]{1,0:T(8,128)(2,1)S(1)}, bf16[520,256]{1,0:T(8,128)(2,1)S(1)}, u32[]{:S(2)}, u32[]{:S(2)}) collective-permute-start(bf16[520,256]{1,0:T(8,128)(2,1)S(1)} %broadcast_select_fusion.1), channel_id=1, source_target_pairs={{0,1},{1,0},{2,3},{3,2},{4,5},{5,4},{6,7},{7,6},{8,9},{9,8},{10,11... | collective-permute-start | bytes 798728 | tf_op jit(solution)/shard_map/ppermute | solution.py:170
  46.8 13.2 %collective-permute-start.10 = (bf16[520,256]{1,0:T(8,128)(2,1)S(1)}, bf16[520,256]{1,0:T(8,128)(2,1)S(1)}, u32[]{:S(2)}, u32[]{:S(2)}) collective-permute-start(bf16[520,256]{1,0:T(8,128)(2,1)S(1)} %pad_select_fusion), channel_id=1, source_target_pairs={{1,0},{2,3},{3,2},{5,4},{6,7},{7,6},{9,8},{10,11},{11,10},{13,12},... | collective-permute-start | bytes 798728 | tf_op jit(solution)/shard_map/ppermute | solution.py:170
  50.2 9.8 %collective-permute-start.14 = (bf16[520,256]{1,0:T(8,128)(2,1)S(1)}, bf16[520,256]{1,0:T(8,128)(2,1)S(1)}, u32[]{:S(2)}, u32[]{:S(2)}) collective-permute-start(bf16[520,256]{1,0:T(8,128)(2,1)S(1)} %collective-permute-done.13.refs_5_), channel_id=1, source_target_pairs={{0,2},{1,3},{4,6},{5,7},{8,10},{9,11},{12,14},{13,15},{16,18},{17,... | collective-permute-start | bytes 798728 | tf_op jit(solution)/shard_map/ppermute | solution.py:170
  51.7 8.3 %collective-permute-start.7 = (bf16[512,256]{1,0:T(8,128)(2,1)S(1)}, bf16[512,256]{1,0:T(8,128)(2,1)S(1)}, u32[]{:S(2)}, u32[]{:S(2)}) collective-permute-start(bf16[512,256]{1,0:T(8,128)(2,1)S(1)} %broadcast_select_fusion.4), channel_id=1, source_target_pairs={{1,13},{2,14},{3,15},{5,1},{6,2},{7,3},{9,5},{10,6},{11,7},{13,9},... | collective-permute-start | bytes 786440 | tf_op jit(solution)/shard_map/ppermute | solution.py:170

commit v3 on v2

--- a/solution.py
+++ b/solution.py
@@ -73,24 +73,24 @@
     column = lax.axis_index("sc")
 
     place = lax.broadcasted_iota(jnp.int32, offsets_ref.shape, 1)
-    wanted, slots = [], []
+    wanted, keys = [], []
     for entry in entries:
         offset, use = entry(column)
         use = jnp.logical_and(use, jnp.logical_and(offset >= 0, offset < slot_count))
 
-        hit = offsets_ref[...] == offset
         wanted.append(use)
-        slots.append(jnp.sum(jnp.where(hit, place, 0)))
-
-    def copy_out(i, f):
+        keys.append(offset)
+
+    def copy_out(i, f, slot):
         return pltpu.make_async_copy(
-            stage.at[i, f], out_ref.at[f, 0, slots[i]], sems.at[i, f]
+            stage.at[i, f], out_ref.at[f, 0, slot], sems.at[i, f]
         )
 
     for i in range(pair_count):
 
         @pl.when(wanted[i])
         def _(i=i):
+            slot = jnp.sum(jnp.where(offsets_ref[...] == keys[i], place, 0))
             parts = imags[i][pl.ds(bins * rows, GAIN_ROWS), :rows].astype(jnp.float32)
             gain = parts[0:1] + parts[1:2] + parts[2:3]
             weight = weight_ref[...] * gain
@@ -105,14 +105,14 @@
                 imag = four[rows:, :rows] - four[:rows, rows:]
                 stage[i, f, :, :rows] = real * weight
                 stage[i, f, :, rows:] = imag * weight
-                copy_out(i, f).start()
+                copy_out(i, f, slot).start()
 
     for i in range(pair_count):
 
         @pl.when(wanted[i])
         def _(i=i):
             for f in range(bins):
-                copy_out(i, f).wait()
+                copy_out(i, f, 0).wait()
 
 
 def products(offsets, own, weight, group, out_shape, out):

time: 61.6 us -> 61.5 us (level)
  no operation moved by 1% of the time
where the time goes in v3:
time: 61.5 us; the launch traced here: 61.2 us
  starting transfers between devices  29.3 us (48%)
  waiting for transfers between devices  23.7 us (39%)
  Pallas kernels  5.89 us (10%)
  local copies, waits for them, and re-layouts  1.9 us (3%)
    ppermute x19, starting transfers between devices, send(): return lax.ppermute(value, BLOCKS, links)  29.2 us
    ppermute x19, waiting for transfers between devices, send(): return lax.ppermute(value, BLOCKS, links)  22.5 us
    pallas_call x3, Pallas kernels, products(): pl.pallas_call(functools.partial(product_kernel, [entry for _, entry in g...  5.56 us
    unnamed x6, local copies, waits for them, and re-layouts  1.9 us
  transfers between devices with their start and end apart: 20, of which 9 were waited for; matrix products, arithmetic and copies ran while one was open for 0% of the time, Pallas kernels for 8%

profile of v3, /device:TPU:10, one launch (start us, length us, event | category | flops | bytes accessed | tf_op | source)
XLA Modules:
  0.0 61.2 jit_solution(8665048885556270522)
XLA Ops:
  0.0 0.4 collective-permute-start.2
  0.5 0.9 %copy-done = bf16[4,128,256]{2,1,0:T(8,128)(2,1)S(1)} copy-done((bf16[4,128,256]{2,1,0:T(8,128)(2,1)S(1)}, bf16[4,128,256]{2,1,0:T(8,128)(2,1)}, u32[]{:S(2)}) %copy-start) | copy-done | bytes 262168
  1.4 0.9 %copy-done.1 = bf16[4,128,256]{2,1,0:T(8,128)(2,1)S(1)} copy-done((bf16[4,128,256]{2,1,0:T(8,128)(2,1)S(1)}, bf16[4,128,256]{2,1,0:T(8,128)(2,1)}, u32[]{:S(2)}) %copy-start.1) | copy-done | bytes 262168
  2.4 0.2 power.1
  2.6 0.1 collective-permute-start
  2.7 1.2 %collective-permute-done.other_ref = f32[8,128]{1,0:T(8,128)S(1)} collective-permute-done((f32[8,128]{1,0:T(8,128)S(1)}, f32[8,128]{1,0:T(8,128)S(1)}, u32[]{:S(2)}, u32[]{:S(2)}) %collective-permute-start) | collective-permute-done | bytes 4128 | tf_op jit(solution)/shard_map/ppermute | solution.py:201
  3.8 0.1 cat.1
  3.9 3.7 %collective-permute-start.11 = (bf16[520,256]{1,0:T(8,128)(2,1)S(1)}, bf16[520,256]{1,0:T(8,128)(2,1)S(1)}, u32[]{:S(2)}, u32[]{:S(2)}) collective-permute-start(bf16[520,256]{1,0:T(8,128)(2,1)S(1)} %get-tuple-element.15.im_ref.refs_6_), channel_id=1, source_target_pairs={{0,12},{1,13},{2,14},{3,15},{4,0},{5,1},{6,2},{7,3},{8,4},{9,5},{1... | collective-permute-start | bytes 798728 | tf_op jit(solution)/shard_map/ppermute | solution.py:170
  7.6 1.3 %collective-permute-start.4 = (bf16[512,256]{1,0:T(8,128)(2,1)S(1)}, bf16[512,256]{1,0:T(8,128)(2,1)S(1)}, u32[]{:S(2)}, u32[]{:S(2)}) collective-permute-start(bf16[512,256]{1,0:T(8,128)(2,1)S(1)} %get-tuple-element.12.re_ref.refs_0_), channel_id=1, source_target_pairs={{2,0},{3,1},{6,4},{7,5},{10,8},{11,9},{14,12},{15,13},{18,16},{19,... | collective-permute-start | bytes 786440 | tf_op jit(solution)/shard_map/ppermute | solution.py:170
  8.9 0.5 collective-permute-done.2.refs_1_
  9.4 2.2 %collective-permute-start.3 = (bf16[512,256]{1,0:T(8,128)(2,1)S(1)}, bf16[512,256]{1,0:T(8,128)(2,1)S(1)}, u32[]{:S(2)}, u32[]{:S(2)}) collective-permute-start(bf16[512,256]{1,0:T(8,128)(2,1)S(1)} %collective-permute-done.2.refs_1_), channel_id=1, source_target_pairs={{0,2},{1,3},{2,0},{3,1},{4,6},{5,7},{6,4},{7,5},{8,10},{9,11},{10,... | collective-permute-start | bytes 786440 | tf_op jit(solution)/shard_map/ppermute | solution.py:170
  11.6 0.5 collective-permute-start.6
  12.1 1.0 %collective-permute-start.8 = (bf16[512,256]{1,0:T(8,128)(2,1)S(1)}, bf16[512,256]{1,0:T(8,128)(2,1)S(1)}, u32[]{:S(2)}, u32[]{:S(2)}) collective-permute-start(bf16[512,256]{1,0:T(8,128)(2,1)S(1)} %collective-permute-done.2.refs_1_), channel_id=1, source_target_pairs={{0,12},{1,13},{2,14},{3,15},{4,0},{5,1},{6,2},{7,3},{8,4},{9,5},{1... | collective-permute-start | bytes 786440 | tf_op jit(solution)/shard_map/ppermute | solution.py:170
  13.1 5.5 %collective-permute-done.4.refs_2_ = bf16[512,256]{1,0:T(8,128)(2,1)S(1)} collective-permute-done((bf16[512,256]{1,0:T(8,128)(2,1)S(1)}, bf16[512,256]{1,0:T(8,128)(2,1)S(1)}, u32[]{:S(2)}, u32[]{:S(2)}) %collective-permute-start.4) | collective-permute-done | bytes 262176 | tf_op jit(solution)/shard_map/ppermute | solution.py:170
  18.6 2.4 %collective-permute-start.1 = (bf16[512,256]{1,0:T(8,128)(2,1)S(1)}, bf16[512,256]{1,0:T(8,128)(2,1)S(1)}, u32[]{:S(2)}, u32[]{:S(2)}) collective-permute-start(bf16[512,256]{1,0:T(8,128)(2,1)S(1)} %get-tuple-element.12.re_ref.refs_0_), channel_id=1, source_target_pairs={{1,0},{3,2},{5,4},{7,6},{9,8},{11,10},{13,12},{15,14},{17,16},{19,... | collective-permute-start | bytes 786440 | tf_op jit(solution)/shard_map/ppermute | solution.py:170
  21.1 0.0 collective-permute-done.11.refs_7_
  21.1 0.1 collective-permute-start.12
  21.2 2.0 %collective-permute-done.3.refs_4_ = bf16[512,256]{1,0:T(8,128)(2,1)S(1)} collective-permute-done((bf16[512,256]{1,0:T(8,128)(2,1)S(1)}, bf16[512,256]{1,0:T(8,128)(2,1)S(1)}, u32[]{:S(2)}, u32[]{:S(2)}) %collective-permute-start.3) | collective-permute-done | bytes 262176 | tf_op jit(solution)/shard_map/ppermute | solution.py:170
  23.2 0.4 collective-permute-start.18
  23.7 0.0 collective-permute-done.6.refs_3_
  23.7 1.3 %collective-permute-start.16 = (bf16[520,256]{1,0:T(8,128)(2,1)S(1)}, bf16[520,256]{1,0:T(8,128)(2,1)S(1)}, u32[]{:S(2)}, u32[]{:S(2)}) collective-permute-start(bf16[520,256]{1,0:T(8,128)(2,1)S(1)} %get-tuple-element.15.im_ref.refs_6_), channel_id=1, source_target_pairs={{2,0},{3,1},{6,4},{7,5},{10,8},{11,9},{14,12},{15,13},{18,16},{19,... | collective-permute-start | bytes 798728 | tf_op jit(solution)/shard_map/ppermute | solution.py:170
  25.0 0.0 collective-permute-done.8.refs_5_
  25.0 2.7 %collective-permute-start.15 = (bf16[520,256]{1,0:T(8,128)(2,1)S(1)}, bf16[520,256]{1,0:T(8,128)(2,1)S(1)}, u32[]{:S(2)}, u32[]{:S(2)}) collective-permute-start(bf16[520,256]{1,0:T(8,128)(2,1)S(1)} %collective-permute-done.11.refs_7_), channel_id=1, source_target_pairs={{0,2},{1,3},{2,0},{3,1},{4,6},{5,7},{6,4},{7,5},{8,10},{9,11},{10,... | collective-permute-start | bytes 798728 | tf_op jit(solution)/shard_map/ppermute | solution.py:170
  27.7 3.0 %collective-permute-done.12.refs_9_ = bf16[520,256]{1,0:T(8,128)(2,1)S(1)} collective-permute-done((bf16[520,256]{1,0:T(8,128)(2,1)S(1)}, bf16[520,256]{1,0:T(8,128)(2,1)S(1)}, u32[]{:S(2)}, u32[]{:S(2)}) %collective-permute-start.12) | collective-permute-done | bytes 266272 | tf_op jit(solution)/shard_map/ppermute | solution.py:170
  30.8 2.5 %collective-permute-start.5 = (bf16[512,256]{1,0:T(8,128)(2,1)S(1)}, bf16[512,256]{1,0:T(8,128)(2,1)S(1)}, u32[]{:S(2)}, u32[]{:S(2)}) collective-permute-start(bf16[512,256]{1,0:T(8,128)(2,1)S(1)} %broadcast_select_fusion.3), channel_id=1, source_target_pairs={{0,1},{1,0},{2,3},{3,2},{4,5},{5,4},{6,7},{7,6},{8,9},{9,8},{10,11... | collective-permute-start | bytes 786440 | tf_op jit(solution)/shard_map/ppermute | solution.py:170
  33.2 0.0 collective-permute-done.18.refs_11_
  33.2 0.0 collective-permute-start.9
  33.3 1.6 %collective-permute-done.16.refs_8_ = bf16[520,256]{1,0:T(8,128)(2,1)S(1)} collective-permute-done((bf16[520,256]{1,0:T(8,128)(2,1)S(1)}, bf16[520,256]{1,0:T(8,128)(2,1)S(1)}, u32[]{:S(2)}, u32[]{:S(2)}) %collective-permute-start.16) | collective-permute-done | bytes 266272 | tf_op jit(solution)/shard_map/ppermute | solution.py:170
  34.8 0.5 collective-permute-start.19
  35.4 5.2 %collective-permute-done.15.refs_10_ = bf16[520,256]{1,0:T(8,128)(2,1)S(1)} collective-permute-done((bf16[520,256]{1,0:T(8,128)(2,1)S(1)}, bf16[520,256]{1,0:T(8,128)(2,1)S(1)}, u32[]{:S(2)}, u32[]{:S(2)}) %collective-permute-start.15) | collective-permute-done | bytes 266272 | tf_op jit(solution)/shard_map/ppermute | solution.py:170
  40.5 2.3 %collective-permute-start.13 = (bf16[520,256]{1,0:T(8,128)(2,1)S(1)}, bf16[520,256]{1,0:T(8,128)(2,1)S(1)}, u32[]{:S(2)}, u32[]{:S(2)}) collective-permute-start(bf16[520,256]{1,0:T(8,128)(2,1)S(1)} %collective-permute-done.12.refs_9_), channel_id=1, source_target_pairs={{0,12},{1,13},{3,15},{4,0},{5,1},{7,3},{8,4},{9,5},{11,7},{12,8},{... | collective-permute-start | bytes 798728 | tf_op jit(solution)/shard_map/ppermute | solution.py:170
  42.9 3.2 %collective-permute-done.9.refs_1_ = bf16[512,256]{1,0:T(8,128)(2,1)S(1)} collective-permute-done((bf16[512,256]{1,0:T(8,128)(2,1)S(1)}, bf16[512,256]{1,0:T(8,128)(2,1)S(1)}, u32[]{:S(2)}, u32[]{:S(2)}) %collective-permute-start.9) | collective-permute-done | bytes 262176 | tf_op jit(solution)/shard_map/ppermute | solution.py:170
  46.2 0.5 collective-permute-start.17
  46.7 0.1 pad_select_fusion
  46.8 0.0 collective-permute-done.5.refs_0_
  46.8 3.4 %collective-permute-start.10 = (bf16[520,256]{1,0:T(8,128)(2,1)S(1)}, bf16[520,256]{1,0:T(8,128)(2,1)S(1)}, u32[]{:S(2)}, u32[]{:S(2)}) collective-permute-start(bf16[520,256]{1,0:T(8,128)(2,1)S(1)} %pad_select_fusion), channel_id=1, source_target_pairs={{1,0},{2,3},{3,2},{5,4},{6,7},{7,6},{9,8},{10,11},{11,10},{13,12},... | collective-permute-start | bytes 798728 | tf_op jit(solution)/shard_map/ppermute | solution.py:170
  50.2 0.0 collective-permute-done.13.refs_5_
  50.2 1.5 %collective-permute-start.14 = (bf16[520,256]{1,0:T(8,128)(2,1)S(1)}, bf16[520,256]{1,0:T(8,128)(2,1)S(1)}, u32[]{:S(2)}, u32[]{:S(2)}) collective-permute-start(bf16[520,256]{1,0:T(8,128)(2,1)S(1)} %collective-permute-done.13.refs_5_), channel_id=1, source_target_pairs={{0,2},{1,3},{4,6},{5,7},{8,10},{9,11},{12,14},{13,15},{16,18},{17,... | collective-permute-start | bytes 798728 | tf_op jit(solution)/shard_map/ppermute | solution.py:170
  51.7 0.0 collective-permute-done.19.refs_3_
  51.7 2.4 %collective-permute-start.7 = (bf16[512,256]{1,0:T(8,128)(2,1)S(1)}, bf16[512,256]{1,0:T(8,128)(2,1)S(1)}, u32[]{:S(2)}, u32[]{:S(2)}) collective-permute-start(bf16[512,256]{1,0:T(8,128)(2,1)S(1)} %broadcast_select_fusion.4), channel_id=1, source_target_pairs={{1,13},{2,14},{3,15},{5,1},{6,2},{7,3},{9,5},{10,6},{11,7},{13,9},... | collective-permute-start | bytes 786440 | tf_op jit(solution)/shard_map/ppermute | solution.py:170
  54.1 2.8 %shard_map.37.refs_4_ = f32[4,1,9,128,256]{4,3,2,1,0:T(8,128)} custom-call(s32[1,9]{1,0:T(1,128)S(1)} %copy-done.2, bf16[512,256]{1,0:T(8,128)(2,1)S(1)} %get-tuple-element.12.re_ref.refs_0_, bf16[520,256]{1,0:T(8,128)(2,1)S(1)} %get-tuple-element.15.im_ref.refs_6_, f32[128,128]{1,0:T(8,128)S(1)} %get-tuple-element.16.weight_ref, ...), custom_call_target="tpu_custom_call" | custom-call | flops 805306368 | bytes 3145728 | tf_op jit(solution)/shard_map/pallas_call | solution.py:130
  56.9 0.0 collective-permute-done.17.refs_2_
  57.0 1.5 %shard_map.38.refs_8_ = f32[4,1,9,128,256]{4,3,2,1,0:T(8,128)} custom-call(s32[1,9]{1,0:T(1,128)S(1)} %copy-done.2, bf16[512,256]{1,0:T(8,128)(2,1)S(1)} %get-tuple-element.12.re_ref.refs_0_, bf16[520,256]{1,0:T(8,128)(2,1)S(1)} %get-tuple-element.15.im_ref.refs_6_, f32[128,128]{1,0:T(8,128)S(1)} %get-tuple-element.16.weight_ref, ...), custom_call_target="tpu_custom_call", output_to_operand_aliasing={{}: (8, {})} | custom-call | flops 268435456 | bytes 1048576 | tf_op jit(solution)/shard_map/pallas_call | solution.py:130
  58.5 0.0 collective-permute-done.1.refs_0_
  58.5 1.5 %collective-permute-done.7.refs_1_.refs_2_ = bf16[512,256]{1,0:T(8,128)(2,1)S(1)} collective-permute-done((bf16[512,256]{1,0:T(8,128)(2,1)S(1)}, bf16[512,256]{1,0:T(8,128)(2,1)S(1)}, u32[]{:S(2)}, u32[]{:S(2)}) %collective-permute-start.7) | collective-permute-done | bytes 262176 | tf_op jit(solution)/shard_map/ppermute | solution.py:170
  60.0 0.0 collective-permute-done.10.refs_3_.refs_4_
  60.0 0.0 collective-permute-done.14.refs_6_.refs_7_
  60.0 1.2 %shard_map.39 = f32[4,1,9,128,256]{4,3,2,1,0:T(8,128)} custom-call(s32[1,9]{1,0:T(1,128)S(1)} %copy-done.2, bf16[512,256]{1,0:T(8,128)(2,1)S(1)} %get-tuple-element.12.re_ref.refs_0_, bf16[520,256]{1,0:T(8,128)(2,1)S(1)} %get-tuple-element.15.im_ref.refs_6_, f32[128,128]{1,0:T(8,128)S(1)} %get-tuple-element.16.weight_ref, ...), custom_call_target="tpu_custom_call", output_to_operand_aliasing={{}: (12, {})} | custom-call | flops 536870912 | bytes 2097152 | tf_op jit(solution)/shard_map/pallas_call | solution.py:130
  (9 shorter events, 0.2 us)
Async XLA Ops:
  0.0 54.1 %copy-start.2 = (s32[1,9]{1,0:T(1,128)S(1)}, s32[1,9]{1,0:T(1,128)}, u32[]{:S(2)}) copy-start(s32[1,9]{1,0:T(1,128)} %offsets_ref.5) | copy-start | bytes 112
  0.0 9.4 %collective-permute-start.2 = (bf16[512,256]{1,0:T(8,128)(2,1)}, bf16[512,256]{1,0:T(8,128)(2,1)S(1)}, u32[]{:S(2)}, u32[]{:S(2)}) collective-permute-start(bf16[512,256]{1,0:T(8,128)(2,1)} %bitcast.3), channel_id=1, source_target_pairs={{0,12},{1,13},{2,14},{3,15},{4,0},{5,1},{6,2},{7,3},{8,4},{9,5},{1... | collective-permute-start | bytes 786440 | tf_op jit(solution)/shard_map/ppermute | solution.py:170
  0.5 0.9 %copy-start = (bf16[4,128,256]{2,1,0:T(8,128)(2,1)S(1)}, bf16[4,128,256]{2,1,0:T(8,128)(2,1)}, u32[]{:S(2)}) copy-start(bf16[4,128,256]{2,1,0:T(8,128)(2,1)} %param.4) | copy-start | bytes 786436
  1.4 0.9 %copy-start.1 = (bf16[4,128,256]{2,1,0:T(8,128)(2,1)S(1)}, bf16[4,128,256]{2,1,0:T(8,128)(2,1)}, u32[]{:S(2)}) copy-start(bf16[4,128,256]{2,1,0:T(8,128)(2,1)} %param.3) | copy-start | bytes 786436
  2.6 1.2 %collective-permute-start = (f32[8,128]{1,0:T(8,128)S(1)}, f32[8,128]{1,0:T(8,128)S(1)}, u32[]{:S(2)}, u32[]{:S(2)}) collective-permute-start(f32[8,128]{1,0:T(8,128)S(1)} %get-tuple-element.14.mine_ref), channel_id=1, source_target_pairs={{0,16},{16,0},{1,17},{17,1},{2,18},{18,2},{3,19},{19,3},{4,20},{20... | collective-permute-start | bytes 12296 | tf_op jit(solution)/shard_map/ppermute | solution.py:201
  3.9 17.2 %collective-permute-start.11 = (bf16[520,256]{1,0:T(8,128)(2,1)S(1)}, bf16[520,256]{1,0:T(8,128)(2,1)S(1)}, u32[]{:S(2)}, u32[]{:S(2)}) collective-permute-start(bf16[520,256]{1,0:T(8,128)(2,1)S(1)} %get-tuple-element.15.im_ref.refs_6_), channel_id=1, source_target_pairs={{0,12},{1,13},{2,14},{3,15},{4,0},{5,1},{6,2},{7,3},{8,4},{9,5},{1... | collective-permute-start | bytes 798728 | tf_op jit(solution)/shard_map/ppermute | solution.py:170
  7.6 11.1 %collective-permute-start.4 = (bf16[512,256]{1,0:T(8,128)(2,1)S(1)}, bf16[512,256]{1,0:T(8,128)(2,1)S(1)}, u32[]{:S(2)}, u32[]{:S(2)}) collective-permute-start(bf16[512,256]{1,0:T(8,128)(2,1)S(1)} %get-tuple-element.12.re_ref.refs_0_), channel_id=1, source_target_pairs={{2,0},{3,1},{6,4},{7,5},{10,8},{11,9},{14,12},{15,13},{18,16},{19,... | collective-permute-start | bytes 786440 | tf_op jit(solution)/shard_map/ppermute | solution.py:170
  9.4 13.8 %collective-permute-start.3 = (bf16[512,256]{1,0:T(8,128)(2,1)S(1)}, bf16[512,256]{1,0:T(8,128)(2,1)S(1)}, u32[]{:S(2)}, u32[]{:S(2)}) collective-permute-start(bf16[512,256]{1,0:T(8,128)(2,1)S(1)} %collective-permute-done.2.refs_1_), channel_id=1, source_target_pairs={{0,2},{1,3},{2,0},{3,1},{4,6},{5,7},{6,4},{7,5},{8,10},{9,11},{10,... | collective-permute-start | bytes 786440 | tf_op jit(solution)/shard_map/ppermute | solution.py:170
  11.6 12.1 %collective-permute-start.6 = (bf16[512,256]{1,0:T(8,128)(2,1)S(1)}, bf16[512,256]{1,0:T(8,128)(2,1)S(1)}, u32[]{:S(2)}, u32[]{:S(2)}) collective-permute-start(bf16[512,256]{1,0:T(8,128)(2,1)S(1)} %collective-permute-done.2.refs_1_), channel_id=1, source_target_pairs={{0,1},{1,0},{2,3},{3,2},{4,5},{5,4},{6,7},{7,6},{8,9},{9,8},{10,11... | collective-permute-start | bytes 786440 | tf_op jit(solution)/shard_map/ppermute | solution.py:170
  12.1 12.8 %collective-permute-start.8 = (bf16[512,256]{1,0:T(8,128)(2,1)S(1)}, bf16[512,256]{1,0:T(8,128)(2,1)S(1)}, u32[]{:S(2)}, u32[]{:S(2)}) collective-permute-start(bf16[512,256]{1,0:T(8,128)(2,1)S(1)} %collective-permute-done.2.refs_1_), channel_id=1, source_target_pairs={{0,12},{1,13},{2,14},{3,15},{4,0},{5,1},{6,2},{7,3},{8,4},{9,5},{1... | collective-permute-start | bytes 786440 | tf_op jit(solution)/shard_map/ppermute | solution.py:170
  18.6 39.8 %collective-permute-start.1 = (bf16[512,256]{1,0:T(8,128)(2,1)S(1)}, bf16[512,256]{1,0:T(8,128)(2,1)S(1)}, u32[]{:S(2)}, u32[]{:S(2)}) collective-permute-start(bf16[512,256]{1,0:T(8,128)(2,1)S(1)} %get-tuple-element.12.re_ref.refs_0_), channel_id=1, source_target_pairs={{1,0},{3,2},{5,4},{7,6},{9,8},{11,10},{13,12},{15,14},{17,16},{19,... | collective-permute-start | bytes 786440 | tf_op jit(solution)/shard_map/ppermute | solution.py:170
  21.1 9.7 %collective-permute-start.12 = (bf16[520,256]{1,0:T(8,128)(2,1)S(1)}, bf16[520,256]{1,0:T(8,128)(2,1)S(1)}, u32[]{:S(2)}, u32[]{:S(2)}) collective-permute-start(bf16[520,256]{1,0:T(8,128)(2,1)S(1)} %collective-permute-done.11.refs_7_), channel_id=1, source_target_pairs={{0,1},{1,0},{2,3},{3,2},{4,5},{5,4},{6,7},{7,6},{8,9},{9,8},{10,11... | collective-permute-start | bytes 798728 | tf_op jit(solution)/shard_map/ppermute | solution.py:170
  23.2 10.1 %collective-permute-start.18 = (bf16[520,256]{1,0:T(8,128)(2,1)S(1)}, bf16[520,256]{1,0:T(8,128)(2,1)S(1)}, u32[]{:S(2)}, u32[]{:S(2)}) collective-permute-start(bf16[520,256]{1,0:T(8,128)(2,1)S(1)} %collective-permute-done.11.refs_7_), channel_id=1, source_target_pairs={{0,12},{1,13},{2,14},{3,15},{4,0},{5,1},{6,2},{7,3},{8,4},{9,5},{1... | collective-permute-start | bytes 798728 | tf_op jit(solution)/shard_map/ppermute | solution.py:170
  23.7 11.2 %collective-permute-start.16 = (bf16[520,256]{1,0:T(8,128)(2,1)S(1)}, bf16[520,256]{1,0:T(8,128)(2,1)S(1)}, u32[]{:S(2)}, u32[]{:S(2)}) collective-permute-start(bf16[520,256]{1,0:T(8,128)(2,1)S(1)} %get-tuple-element.15.im_ref.refs_6_), channel_id=1, source_target_pairs={{2,0},{3,1},{6,4},{7,5},{10,8},{11,9},{14,12},{15,13},{18,16},{19,... | collective-permute-start | bytes 798728 | tf_op jit(solution)/shard_map/ppermute | solution.py:170
  25.0 15.6 %collective-permute-start.15 = (bf16[520,256]{1,0:T(8,128)(2,1)S(1)}, bf16[520,256]{1,0:T(8,128)(2,1)S(1)}, u32[]{:S(2)}, u32[]{:S(2)}) collective-permute-start(bf16[520,256]{1,0:T(8,128)(2,1)S(1)} %collective-permute-done.11.refs_7_), channel_id=1, source_target_pairs={{0,2},{1,3},{2,0},{3,1},{4,6},{5,7},{6,4},{7,5},{8,10},{9,11},{10,... | collective-permute-start | bytes 798728 | tf_op jit(solution)/shard_map/ppermute | solution.py:170
  30.8 16.0 %collective-permute-start.5 = (bf16[512,256]{1,0:T(8,128)(2,1)S(1)}, bf16[512,256]{1,0:T(8,128)(2,1)S(1)}, u32[]{:S(2)}, u32[]{:S(2)}) collective-permute-start(bf16[512,256]{1,0:T(8,128)(2,1)S(1)} %broadcast_select_fusion.3), channel_id=1, source_target_pairs={{0,1},{1,0},{2,3},{3,2},{4,5},{5,4},{6,7},{7,6},{8,9},{9,8},{10,11... | collective-permute-start | bytes 786440 | tf_op jit(solution)/shard_map/ppermute | solution.py:170
  33.2 12.9 %collective-permute-start.9 = (bf16[512,256]{1,0:T(8,128)(2,1)S(1)}, bf16[512,256]{1,0:T(8,128)(2,1)S(1)}, u32[]{:S(2)}, u32[]{:S(2)}) collective-permute-start(bf16[512,256]{1,0:T(8,128)(2,1)S(1)} %broadcast_select_fusion.2), channel_id=1, source_target_pairs={{0,2},{1,3},{2,0},{3,1},{4,6},{5,7},{6,4},{7,5},{8,10},{9,11},{10,... | collective-permute-start | bytes 786440 | tf_op jit(solution)/shard_map/ppermute | solution.py:170
  34.8 16.9 %collective-permute-start.19 = (bf16[520,256]{1,0:T(8,128)(2,1)S(1)}, bf16[520,256]{1,0:T(8,128)(2,1)S(1)}, u32[]{:S(2)}, u32[]{:S(2)}) collective-permute-start(bf16[520,256]{1,0:T(8,128)(2,1)S(1)} %broadcast_select_fusion), channel_id=1, source_target_pairs={{0,2},{1,3},{2,0},{3,1},{4,6},{5,7},{6,4},{7,5},{8,10},{9,11},{10,... | collective-permute-start | bytes 798728 | tf_op jit(solution)/shard_map/ppermute | solution.py:170
  40.5 9.7 %collective-permute-start.13 = (bf16[520,256]{1,0:T(8,128)(2,1)S(1)}, bf16[520,256]{1,0:T(8,128)(2,1)S(1)}, u32[]{:S(2)}, u32[]{:S(2)}) collective-permute-start(bf16[520,256]{1,0:T(8,128)(2,1)S(1)} %collective-permute-done.12.refs_9_), channel_id=1, source_target_pairs={{0,12},{1,13},{3,15},{4,0},{5,1},{7,3},{8,4},{9,5},{11,7},{12,8},{... | collective-permute-start | bytes 798728 | tf_op jit(solution)/shard_map/ppermute | solution.py:170
  46.2 10.8 %collective-permute-start.17 = (bf16[520,256]{1,0:T(8,128)(2,1)S(1)}, bf16[520,256]{1,0:T(8,128)(2,1)S(1)}, u32[]{:S(2)}, u32[]{:S(2)}) collective-permute-start(bf16[520,256]{1,0:T(8,128)(2,1)S(1)} %broadcast_select_fusion.1), channel_id=1, source_target_pairs={{0,1},{1,0},{2,3},{3,2},{4,5},{5,4},{6,7},{7,6},{8,9},{9,8},{10,11... | collective-permute-start | bytes 798728 | tf_op jit(solution)/shard_map/ppermute | solution.py:170
  46.8 13.2 %collective-permute-start.10 = (bf16[520,256]{1,0:T(8,128)(2,1)S(1)}, bf16[520,256]{1,0:T(8,128)(2,1)S(1)}, u32[]{:S(2)}, u32[]{:S(2)}) collective-permute-start(bf16[520,256]{1,0:T(8,128)(2,1)S(1)} %pad_select_fusion), channel_id=1, source_target_pairs={{1,0},{2,3},{3,2},{5,4},{6,7},{7,6},{9,8},{10,11},{11,10},{13,12},... | collective-permute-start | bytes 798728 | tf_op jit(solution)/shard_map/ppermute | solution.py:170
  50.2 9.8 %collective-permute-start.14 = (bf16[520,256]{1,0:T(8,128)(2,1)S(1)}, bf16[520,256]{1,0:T(8,128)(2,1)S(1)}, u32[]{:S(2)}, u32[]{:S(2)}) collective-permute-start(bf16[520,256]{1,0:T(8,128)(2,1)S(1)} %collective-permute-done.13.refs_5_), channel_id=1, source_target_pairs={{0,2},{1,3},{4,6},{5,7},{8,10},{9,11},{12,14},{13,15},{16,18},{17,... | collective-permute-start | bytes 798728 | tf_op jit(solution)/shard_map/ppermute | solution.py:170
  51.7 8.3 %collective-permute-start.7 = (bf16[512,256]{1,0:T(8,128)(2,1)S(1)}, bf16[512,256]{1,0:T(8,128)(2,1)S(1)}, u32[]{:S(2)}, u32[]{:S(2)}) collective-permute-start(bf16[512,256]{1,0:T(8,128)(2,1)S(1)} %broadcast_select_fusion.4), channel_id=1, source_target_pairs={{1,13},{2,14},{3,15},{5,1},{6,2},{7,3},{9,5},{10,6},{11,7},{13,9},... | collective-permute-start | bytes 786440 | tf_op jit(solution)/shard_map/ppermute | solution.py:170
